TPU v7x, 32 devices: a whole 2x2x4 slice. The times are simulated.
32 devices in a mesh: blk: 4 (over y, core), sub: 2 (over x), kv: 4 (over z).
Axes of the slice: x: 2, y: 2, z: 4, core: 2. Of those that a mesh axis runs over, the one named last changes fastest.
Arguments:
- queries: bfloat16 [4, 8192], P('blk', 'kv'), may hold values from -64 to 64
- cache_keys: bfloat16 [1024, 1024], P(('blk', 'sub'), 'kv'), may hold values from -8 to 8
- cache_values: bfloat16 [1024, 1024], P(('blk', 'sub'), 'kv'), may hold values from -6 to 6
- cache_places: int32 [1024], P(('blk', 'sub')), may hold values from 0 to 1023, as said below
- span_start: int32 [1], replicated, may hold values from 0 to 1020
Outputs:
- attended: bfloat16 [4, 8192], P('blk', 'kv')
- peak_logits: float32 [4, 64], P('blk', 'kv')
Inputs may be any that keep to these rules, and one draw needn't show every extreme that they name: `cache_places`: a permutation of 0 to 1023.
All inputs are finite; a program needn't handle non-finite values.
Results may differ from a plain program's by a relative error of at most 0.004.
Values may be sent and summed in bfloat16 or wider, within the bound.
No kernel may reach another device: no remote copies, remote signals or barrier semaphores. Data moves between devices by JAX's collectives and lax.ppermute only.
A program may use at most 64 MiB of HBM per device.

v0:
```python
import math

import jax
import jax.numpy as jnp
from jax import lax
from jax.sharding import PartitionSpec as P

HD = 128


def attend_share(query_heads, key_heads, place_rows, query_places):
    scores = jnp.einsum(
        "tgjd,rgd->tgjr", query_heads, key_heads, preferred_element_type=jnp.float32
    )
    scores = scores * (1.0 / math.sqrt(HD))
    visible = (place_rows[None, :] <= query_places[:, None]).astype(jnp.int32)
    shown = (visible > 0)[:, None, None, :]
    scores = jnp.where(shown, scores, -1e30)
    return (scores, shown)


def on_device(queries, cache_keys, cache_values, cache_places, span_start):
    heads_here = queries.shape[1] // HD
    kv_here = cache_keys.shape[1] // HD
    group_size = heads_here // kv_here
    rows_here = queries.shape[0]
    owner = lax.axis_index("blk")
    gathered = lax.all_gather(queries, "blk", axis=0, tiled=True)
    key_rows, value_rows, place_rows = (cache_keys, cache_values, cache_places)
    count = gathered.shape[0]
    query_places = span_start[0] + jnp.arange(count, dtype=jnp.int32)
    query_heads = gathered.reshape(count, kv_here, group_size, HD)
    key_heads = key_rows.reshape(-1, kv_here, HD)
    value_heads = value_rows.reshape(-1, kv_here, HD)
    scores, shown = attend_share(query_heads, key_heads, place_rows, query_places)
    local_peak = jnp.max(scores, axis=3)
    peaks = lax.pmax(local_peak, ("blk", "sub"))
    weights = jnp.where(shown, jnp.exp(scores - peaks[..., None]), 0.0).astype(jnp.bfloat16)
    numerator = jnp.einsum(
        "tgjr,rgd->tgjd", weights, value_heads, preferred_element_type=jnp.float32
    )
    denominator = jnp.sum(weights, axis=3, dtype=jnp.float32)
    numerator, denominator = (
        lax.psum_scatter(numerator, "blk", scatter_dimension=0, tiled=True),
        lax.psum_scatter(denominator, "blk", scatter_dimension=0, tiled=True),
    )
    numerator, denominator = lax.psum((numerator, denominator), "sub")
    attended = (
        (numerator / denominator[..., None])
        .reshape(rows_here, heads_here * HD)
        .astype(jnp.bfloat16)
    )
    own_peaks = lax.dynamic_slice_in_dim(peaks, owner * rows_here, rows_here, 0).reshape(
        rows_here, heads_here
    )
    return (attended, own_peaks)


def solution(mesh):
    placed = (
        P("blk", "kv"),
        P(("blk", "sub"), "kv"),
        P(("blk", "sub"), "kv"),
        P(("blk", "sub")),
        P(),
    )
    return jax.shard_map(
        on_device,
        mesh=mesh,
        in_specs=placed,
        out_specs=(P("blk", "kv"), P("blk", "kv")),
        check_vma=False,
    )
```

profile of v0, /device:TPU:0, one launch (start us, length us, event | category | flops | bytes accessed | tf_op | source)
XLA Modules:
  0.0 44.3 jit_solution(6689250681713933632)
XLA Ops:
  1.3 0.0 copy-start.2
  1.3 0.6 %copy-done.2 = s32[128]{0:T(128)S(1)} copy-done((s32[128]{0:T(128)S(1)}, s32[128]{0:T(128)}, u32[]{:S(2)}) %copy-start.2) | copy-done | bytes 536
  1.9 0.1 convert_compare_fusion
  2.0 0.0 copy-start.1
  2.0 0.9 %reshape.63 = bf16[128,2,128]{2,1,0:T(2,128)(2,1)S(1)} reshape(bf16[128,256]{1,0:T(8,128)(2,1)} %param.6) | data formatting | bytes 131072 | tf_op jit(solution)/shard_map/reshape | solution.py:33
  2.9 0.0 copy-done.1
  2.9 6.2 %all-gather = bf16[4,1,2048]{2,1,0:T(2,128)(2,1)S(1)} all-gather(bf16[1,1,2048]{2,1,0:T(2,128)(2,1)S(1)} %bitcast.29), channel_id=1, replica_groups=mesh['blk'=4,'sub'=2,'kv'=4] {'blk'}, dimensions={0}, use_global_device_ids=true | all-gather | bytes 20480 | tf_op jit(solution)/shard_map/all_gather | solution.py:28
  9.1 0.1 reduce
  9.2 0.0 copy-start
  9.2 0.2 fusion.6
  9.5 14.8 %pmax.7 = f32[4,2,8]{2,0,1:T(4,128)S(1)} all-reduce(f32[4,2,8]{2,0,1:T(4,128)S(1)} %get-tuple-element.6), channel_id=1, replica_groups=mesh['blk'=4,'sub'=2,'kv'=4] {'blk','sub'}, use_global_device_ids=true, to_apply=%region_1.2 | all-reduce | flops 64 | bytes 512 | tf_op jit(solution)/shard_map/pmax | solution.py:37
  24.2 0.2 convert_reduce_fusion
  24.4 0.0 copy-done
  24.4 0.2 convolution_bitcast_fusion
  24.6 10.7 %all-reduce.2 = (f32[4,2,8,128]{3,2,0,1:T(8,128)S(1)}, f32[4,2,8]{2,1,0:T(2,128)S(1)}) all-reduce(f32[4,2,8,128]{3,2,0,1:T(8,128)S(1)} %convolution_bitcast_fusion, f32[4,2,8]{2,1,0:T(2,128)S(1)} %copy.17), channel_id=2, replica_groups=mesh['blk'=4,'sub'=2,'kv'=4] {'blk'}, use_global_device_ids=true, to_apply=%region_2.3.clone | all-reduce | flops 8256 | bytes 66048
  35.4 0.0 copy-start.3
  35.4 0.6 %copy-done.3 = u32[32]{0:T(128)S(1)} copy-done((u32[32]{0:T(128)S(1)}, u32[32]{0:T(128)}, u32[]{:S(2)}) %copy-start.3) | copy-done | bytes 152
  36.0 0.6 %dynamic-slice = u32[1]{0:T(128)} dynamic-slice(u32[32]{0:T(128)S(1)} %copy-done.3, u32[]{:T(128)S(6)} %add.25), dynamic_slice_sizes={1} | dynamic-slice | bytes 12
  36.6 0.6 %constant_dynamic-slice_fusion = f32[1,2,8,128]{3,2,0,1:T(8,128)S(1)} fusion(f32[4,2,8,128]{3,2,0,1:T(8,128)S(1)} %get-tuple-element.2, u32[]{:T(128)} %bitcast.9), kind=kLoop, calls=%fused_computation.14 | loop fusion | bytes 16388
  37.3 0.7 %dynamic-slice_bitcast_fusion = f32[2,8]{1,0:T(2,128)S(1)} fusion(f32[4,2,8]{2,1,0:T(2,128)S(1)} %get-tuple-element.3, u32[]{:T(128)} %bitcast.9), kind=kLoop, calls=%fused_computation.12 | loop fusion | bytes 132 | tf_op jit(solution)/shard_map/div | solution.py:49
  37.9 5.1 %all-reduce.3 = (f32[1,2,8,128]{3,2,0,1:T(8,128)S(1)}, f32[2,8]{1,0:T(2,128)S(1)}) all-reduce(f32[1,2,8,128]{3,2,0,1:T(8,128)S(1)} %constant_dynamic-slice_fusion, f32[2,8]{1,0:T(2,128)S(1)} %dynamic-slice_bitcast_fusion), channel_id=1, replica_groups=mesh['blk'=4,'sub'=2,'kv'=4] {'sub'}, use_global_device_ids=true, to_apply=%region_3.4 | all-reduce | flops 2064 | bytes 16512 | tf_op jit(solution)/shard_map/psum | solution.py:47
  43.0 0.1 divide_convert_fusion
  43.1 0.6 %convert_element_type.31 = bf16[1,2048]{1,0:T(2,128)(2,1)} reshape(bf16[1,2,8,128]{3,2,0,1:T(8,128)(2,1)S(1)} %divide_convert_fusion) | data formatting | bytes 8192 | tf_op jit(solution)/shard_map/convert_element_type | solution.py:51
  43.7 0.6 %reshape.66 = f32[1,16]{1,0:T(1,128)} reshape(f32[2,8]{1,0:T(2,128)S(1)} %dynamic-slice_reduce_fusion) | data formatting | bytes 128 | tf_op jit(solution)/shard_map/reshape | solution.py:53
  (4 shorter events, 0.1 us)
Async XLA Ops:
  1.3 0.7 %copy-start.2 = (s32[128]{0:T(128)S(1)}, s32[128]{0:T(128)}, u32[]{:S(2)}) copy-start(s32[128]{0:T(128)} %param.8) | copy-start | bytes 1540
  2.0 0.9 %copy-start.1 = (bf16[1,2048]{1,0:T(2,128)(2,1)S(1)}, bf16[1,2048]{1,0:T(2,128)(2,1)}, u32[]{:S(2)}) copy-start(bf16[1,2048]{1,0:T(2,128)(2,1)} %param.5) | copy-start | bytes 12292
  9.2 15.2 %copy-start = (bf16[128,256]{1,0:T(8,128)(2,1)S(1)}, bf16[128,256]{1,0:T(8,128)(2,1)}, u32[]{:S(2)}) copy-start(bf16[128,256]{1,0:T(8,128)(2,1)} %param.7) | copy-start | bytes 196612
  35.4 0.7 %copy-start.3 = (u32[32]{0:T(128)S(1)}, u32[32]{0:T(128)}, u32[]{:S(2)}) copy-start(u32[32]{0:T(128)} %constant.21) | copy-start | bytes 388
where the time goes:
time: 44.6 us; the launch traced here: 44.3 us
  blocking collectives  36.8 us (83%)
  local copies, waits for them, and re-layouts  5.31 us (12%)
  between operations  1.37 us (3%)
    pmax x1, blocking collectives, on_device(): peaks = lax.pmax(local_peak, ('blk', 'sub'))  14.8 us
    unnamed x1, blocking collectives  10.7 us
    all_gather x1, blocking collectives, on_device(): gathered = lax.all_gather(queries, 'blk', axis=0, tiled=True)  6.23 us
    psum x1, blocking collectives, on_device(): numerator, denominator = lax.psum((numerator, denominator), 'sub')  5.06 us
    unnamed x10, local copies, waits for them, and re-layouts  2.53 us

commit v1 on v0

v1 whole, which is shorter than its diff:
```python
import functools
import math

import jax
import jax.numpy as jnp
from jax import lax
from jax.experimental import pallas as pl
from jax.experimental.pallas import tpu as pltpu
from jax.sharding import PartitionSpec as P

HD = 128
HIDDEN = -1e30
DIRECT_DEVICES = 16
VMEM_BYTES = 8 * 1024 * 1024


def whole(shape, dtype):
    return jax.ShapeDtypeStruct(shape, dtype)


def params():
    return pltpu.CompilerParams(vmem_limit_bytes=VMEM_BYTES)


def in_vmem(n):
    return [pl.BlockSpec(memory_space=pltpu.VMEM)] * n


def cost(flops):
    return pl.CostEstimate(flops=flops, bytes_accessed=flops // 8, transcendentals=0)


def share_of(query, blocks, shown_rows):
    heads = query.shape[1] // HD
    kv_heads = blocks[0][0].shape[1] // HD
    group = heads // kv_heads
    lane = lax.broadcasted_iota(jnp.int32, (group, HD), 1)
    packed = []
    for j in range(kv_heads):
        first = j * group
        q = jnp.concatenate(
            [query[:, (first + i) * HD : (first + i + 1) * HD] for i in range(group)], axis=0
        )
        scores = [
            jnp.where(
                shown,
                lax.dot_general(
                    q,
                    keys[:, j * HD : (j + 1) * HD],
                    (((1,), (1,)), ((), ())),
                    preferred_element_type=jnp.float32,
                )
                * (1.0 / math.sqrt(HD)),
                HIDDEN,
            )
            for (keys, _), shown in zip(blocks, shown_rows, strict=True)
        ]
        peak = functools.reduce(
            jnp.maximum, [jnp.max(s, axis=1, keepdims=True) for s in scores]
        )
        weights = [
            jnp.where(shown, jnp.exp(s - peak), 0.0).astype(jnp.bfloat16)
            for s, shown in zip(scores, shown_rows, strict=True)
        ]
        denominator = sum(
            jnp.sum(w.astype(jnp.float32), axis=1, keepdims=True) for w in weights
        )
        numerator = sum(
            jnp.dot(w, values[:, j * HD : (j + 1) * HD], preferred_element_type=jnp.float32)
            for w, (_, values) in zip(weights, blocks, strict=True)
        )
        packed.append(
            jnp.concatenate(
                [numerator, jnp.where(lane < HD // 2, peak, denominator)], axis=1
            )
        )
    return jnp.concatenate(packed, axis=0)


def first_kernel(place_ref, query_ref, *refs):
    n = (len(refs) - 2) // 3
    blocks = [(refs[3 * i][...], refs[3 * i + 1][...]) for i in range(n)]
    rows = [refs[3 * i + 2][...] for i in range(n)]
    share_ref, shown_ref = refs[-2:]
    own, other = place_ref[0], place_ref[1]
    share_ref[...] = share_of(query_ref[...], blocks, [r <= own for r in rows])
    for i, r in enumerate(rows):
        shown_ref[i : i + 1] = (r <= other).astype(jnp.int32)


def second_kernel(query_ref, shown_ref, *refs):
    n = (len(refs) - 1) // 2
    blocks = [(refs[2 * i][...], refs[2 * i + 1][...]) for i in range(n)]
    shown = [shown_ref[i : i + 1] > 0 for i in range(n)]
    refs[-1][...] = share_of(query_ref[...], blocks, shown)


def combine_kernel(*refs):
    shares = [r[...] for r in refs[:-2]]
    out_ref, peak_ref = refs[-2:]
    heads = shares[0].shape[0]
    peaks = [s[:, HD : HD + 1] for s in shares]
    peak = functools.reduce(jnp.maximum, peaks)
    scales = [jnp.exp(p - peak) for p in peaks]
    numerator = sum(s[:, :HD] * c for s, c in zip(shares, scales, strict=True))
    denominator = sum(
        s[:, HD + HD // 2 : HD + HD // 2 + 1] * c for s, c in zip(shares, scales, strict=True)
    )
    out = (numerator / denominator).astype(jnp.bfloat16)
    for h in range(heads):
        out_ref[:, h * HD : (h + 1) * HD] = out[h : h + 1]
    row = lax.broadcasted_iota(jnp.int32, (heads, heads), 0)
    column = lax.broadcasted_iota(jnp.int32, (heads, heads), 1)
    peak_ref[...] = jnp.sum(
        jnp.where(row == column, peak, 0.0), axis=0, keepdims=True
    )


def combine(shares, columns):
    heads = shares[0].shape[0]
    return pl.pallas_call(
        combine_kernel,
        out_shape=(whole((1, columns), jnp.bfloat16), whole((1, heads), jnp.float32)),
        in_specs=in_vmem(len(shares)),
        out_specs=tuple(in_vmem(2)),
        compiler_params=params(),
        cost_estimate=cost(1 << 16),
        name="combine",
    )(*shares)


def direct(sizes, queries, cache_keys, cache_values, cache_places, span_start):
    blk, sub = sizes
    columns = queries.shape[1]
    heads = columns // HD
    row_count = cache_keys.shape[0]
    both = ("blk", "sub")

    def swap(value, flip_block, flip_sub):
        pairs = [
            (b * sub + s, (b ^ flip_block) * sub + (s ^ flip_sub))
            for b in range(blk)
            for s in range(sub)
        ]
        return lax.ppermute(value, both, pairs)

    owner = lax.axis_index("blk")
    places = cache_places[None, :]
    other_query = swap(queries, 2, 0)
    far = [swap(x, 1, 0) for x in (cache_keys, cache_values, places)]
    at = span_start[0] + jnp.stack([owner, owner ^ 2]).astype(jnp.int32)
    own_share, shown = pl.pallas_call(
        first_kernel,
        out_shape=(
            whole((heads, 2 * HD), jnp.float32),
            whole((2, row_count), jnp.int32),
        ),
        in_specs=[pl.BlockSpec(memory_space=pltpu.SMEM)] + in_vmem(7),
        out_specs=tuple(in_vmem(2)),
        compiler_params=params(),
        cost_estimate=cost(1 << 22),
        name="own_share",
    )(at, queries, cache_keys, cache_values, places, *far)
    shares = [own_share, swap(own_share, 0, 1)]
    other_share = pl.pallas_call(
        second_kernel,
        out_shape=whole((heads, 2 * HD), jnp.float32),
        in_specs=in_vmem(6),
        out_specs=in_vmem(1)[0],
        compiler_params=params(),
        cost_estimate=cost(1 << 22),
        name="other_share",
    )(other_query, shown, cache_keys, cache_values, *far[:2])
    shares += [swap(other_share, 2, 1), swap(other_share, 2, 0)]
    return combine(shares, columns)


def grouped(queries, cache_keys, cache_values, cache_places, span_start):
    columns = queries.shape[1]
    heads = columns // HD
    kv_heads = cache_keys.shape[1] // HD
    rows_here = queries.shape[0]
    gathered = lax.all_gather(queries, "blk", axis=0, tiled=True)
    count = gathered.shape[0]
    at = span_start[0] + jnp.arange(count, dtype=jnp.int32)
    scores = jnp.einsum(
        "tgjd,rgd->tgjr",
        gathered.reshape(count, kv_heads, heads // kv_heads, HD),
        cache_keys.reshape(-1, kv_heads, HD),
        preferred_element_type=jnp.float32,
    ) * (1.0 / math.sqrt(HD))
    shown = (cache_places[None, :] <= at[:, None])[:, None, None, :]
    scores = jnp.where(shown, scores, HIDDEN)
    peak = jnp.max(scores, axis=3, keepdims=True)
    weights = jnp.where(shown, jnp.exp(scores - peak), 0.0).astype(jnp.bfloat16)
    numerator = jnp.einsum(
        "tgjr,rgd->tgjd",
        weights,
        cache_values.reshape(-1, kv_heads, HD),
        preferred_element_type=jnp.float32,
    )
    denominator = jnp.sum(weights, axis=3, dtype=jnp.float32, keepdims=True)
    shares = jnp.concatenate([numerator, peak, denominator], axis=3)
    shares = shares.reshape(-1, rows_here, heads, HD + 2)
    shares = lax.all_to_all(shares, "blk", 0, 0)
    shares = lax.all_gather(shares, "sub", axis=0, tiled=True)
    peaks = shares[..., HD]
    peak = jnp.max(peaks, axis=0)
    scales = jnp.exp(peaks - peak)
    numerator = jnp.sum(shares[..., :HD] * scales[..., None], axis=0)
    denominator = jnp.sum(shares[..., HD + 1] * scales, axis=0)
    attended = (numerator / denominator[..., None]).astype(jnp.bfloat16)
    return (attended.reshape(rows_here, columns), peak)


def solution(mesh):
    placed = (
        P("blk", "kv"),
        P(("blk", "sub"), "kv"),
        P(("blk", "sub"), "kv"),
        P(("blk", "sub")),
        P(),
    )
    blk, sub = mesh.shape["blk"], mesh.shape["sub"]

    def on_device(queries, *cache):
        if (blk, sub) == (4, 2) and queries.shape[0] == 1:
            return direct((blk, sub), queries, *cache)
        return grouped(queries, *cache)

    return jax.shard_map(
        on_device,
        mesh=mesh,
        in_specs=placed,
        out_specs=(P("blk", "kv"), P("blk", "kv")),
        check_vma=False,
    )
```

time: 44.6 us -> 17.2 us (0.39)
  blocking collectives: 36.8 us -> 0 us
  starting transfers between devices: 0 us -> 7.01 us
  waiting for transfers between devices: 0 us -> 3.64 us
  local copies, waits for them, and re-layouts: 5.31 us -> 2.35 us
  Pallas kernels: 0 us -> 2.53 us
    pmax x1 -> x0, blocking collectives: 14.8 us -> none  [on_device(): peaks = lax.pmax(local_peak, ('blk', 'sub'))]
    unnamed x1 -> x0, blocking collectives: 10.7 us -> none
    ppermute x0 -> x7, starting transfers between devices: none -> 7.01 us  [swap(): return lax.ppermute(value, both, pairs)]
    all_gather x1 -> x0, blocking collectives: 6.23 us -> none  [on_device(): gathered = lax.all_gather(queries, 'blk', axis=0, tiled=True)]
    psum x1 -> x0, blocking collectives: 5.06 us -> none  [on_device(): numerator, denominator = lax.psum((numerator, denominator), 'sub')]
    ppermute x0 -> x7, waiting for transfers between devices: none -> 3.64 us  [swap(): return lax.ppermute(value, both, pairs)]
    pallas_call x0 -> x3, Pallas kernels: none -> 2.53 us  [the longest x1 1.15 us: direct(): pl.pallas_call(first_kernel, out_shape=(whole((heads, 2 * HD), jnp.float3...]
    reshape x3 -> x0, local copies, waits for them, and re-layouts: 1.49 us -> none  [the longest x1 0.87 us: on_device(): key_heads = key_rows.reshape(-1, kv_here, HD)]
  transfers between devices with their start and end apart: 0 -> 7, of which waited for: 0 -> 5; matrix products, arithmetic and copies ran while one was open for 0% -> 0% of each run, Pallas kernels for 0% -> 7%
where the time goes in v1:
time: 17.2 us; the launch traced here: 16.9 us
  starting transfers between devices  7.01 us (41%)
  waiting for transfers between devices  3.64 us (21%)
  Pallas kernels  2.53 us (15%)
  local copies, waits for them, and re-layouts  2.35 us (14%)
  between operations  1.33 us (8%)
    ppermute x7, starting transfers between devices, swap(): return lax.ppermute(value, both, pairs)  7.01 us
    ppermute x7, waiting for transfers between devices, swap(): return lax.ppermute(value, both, pairs)  3.64 us
    unnamed x12, local copies, waits for them, and re-layouts  2.35 us
    pallas_call x1, Pallas kernels, direct(): pl.pallas_call(first_kernel, out_shape=(whole((heads, 2 * HD), jnp.float3...  1.15 us
    pallas_call x1, Pallas kernels, combine(): pl.pallas_call(combine_kernel, out_shape=(whole((1, columns), jnp.bfloat1...  0.77 us
    pallas_call x1, Pallas kernels, direct(): pl.pallas_call(second_kernel, out_shape=whole((heads, 2 * HD), jnp.float3...  0.61 us
  transfers between devices with their start and end apart: 7, of which 5 were waited for; matrix products, arithmetic and copies ran while one was open for 0% of the time, Pallas kernels for 7%

profile of v1, /device:TPU:0, one launch (start us, length us, event | category | flops | bytes accessed | tf_op | source)
XLA Modules:
  0.0 16.9 jit_solution(15331738489498758304)
XLA Ops:
  0.6 0.0 copy-start.5
  0.6 0.6 %copy-done.5 = s32[128]{0:T(128)S(1)} copy-done((s32[128]{0:T(128)S(1)}, s32[128]{0:T(128)}, u32[]{:S(2)}) %copy-start.5) | copy-done | bytes 536
  1.3 0.5 %collective-permute-start.2 = (s32[1,128]{1,0:T(1,128)S(1)}, s32[1,128]{1,0:T(1,128)S(1)}, u32[]{:S(2)}, u32[]{:S(2)}) collective-permute-start(s32[1,128]{1,0:T(1,128)S(1)} %bitcast.5), channel_id=1, source_target_pairs={{0,8},{4,12},{8,0},{12,4},{16,24},{20,28},{24,16},{28,20},{1,9},{5... | collective-permute-start | bytes 1544 | tf_op jit(solution)/shard_map/ppermute | solution.py:145
  1.8 2.5 %collective-permute-start.4 = (bf16[1,2048]{1,0:T(2,128)(2,1)}, bf16[1,2048]{1,0:T(2,128)(2,1)S(1)}, u32[]{:S(2)}, u32[]{:S(2)}) collective-permute-start(bf16[1,2048]{1,0:T(2,128)(2,1)} %query_ref.1), channel_id=1, source_target_pairs={{0,16},{4,20},{8,24},{12,28},{16,0},{20,4},{24,8},{28,12},{1,17},{... | collective-permute-start | bytes 12296 | tf_op jit(solution)/shard_map/ppermute | solution.py:145
  4.3 0.2 %collective-permute-start = (bf16[128,256]{1,0:T(8,128)(2,1)}, bf16[128,256]{1,0:T(8,128)(2,1)S(1)}, u32[]{:S(2)}, u32[]{:S(2)}) collective-permute-start(bf16[128,256]{1,0:T(8,128)(2,1)} %refs_0_.3), channel_id=1, source_target_pairs={{0,8},{4,12},{8,0},{12,4},{16,24},{20,28},{24,16},{28,20},{1,9},{5... | collective-permute-start | bytes 196616 | tf_op jit(solution)/shard_map/ppermute | solution.py:145
  4.5 0.3 %collective-permute-start.1 = (bf16[128,256]{1,0:T(8,128)(2,1)}, bf16[128,256]{1,0:T(8,128)(2,1)S(1)}, u32[]{:S(2)}, u32[]{:S(2)}) collective-permute-start(bf16[128,256]{1,0:T(8,128)(2,1)} %refs_1_.3), channel_id=1, source_target_pairs={{0,8},{4,12},{8,0},{12,4},{16,24},{20,28},{24,16},{28,20},{1,9},{5... | collective-permute-start | bytes 196616 | tf_op jit(solution)/shard_map/ppermute | solution.py:145
  4.8 0.0 copy-start.4
  5.5 0.1 add_add_fusion.place_ref
  5.5 0.0 collective-permute-done.2.refs_5_
  5.5 0.2 %collective-permute-done.refs_3_.refs_2_ = bf16[128,256]{1,0:T(8,128)(2,1)S(1)} collective-permute-done((bf16[128,256]{1,0:T(8,128)(2,1)}, bf16[128,256]{1,0:T(8,128)(2,1)S(1)}, u32[]{:S(2)}, u32[]{:S(2)}) %collective-permute-start) | collective-permute-done | bytes 65568 | tf_op jit(solution)/shard_map/ppermute | solution.py:145
  5.8 0.2 %collective-permute-done.1.refs_4_.refs_3_ = bf16[128,256]{1,0:T(8,128)(2,1)S(1)} collective-permute-done((bf16[128,256]{1,0:T(8,128)(2,1)}, bf16[128,256]{1,0:T(8,128)(2,1)S(1)}, u32[]{:S(2)}, u32[]{:S(2)}) %collective-permute-start.1) | collective-permute-done | bytes 65568 | tf_op jit(solution)/shard_map/ppermute | solution.py:145
  6.0 0.0 copy-done.4
  6.0 0.0 copy-start
  6.0 0.8 %copy-done = bf16[128,256]{1,0:T(8,128)(2,1)S(1)} copy-done((bf16[128,256]{1,0:T(8,128)(2,1)S(1)}, bf16[128,256]{1,0:T(8,128)(2,1)}, u32[]{:S(2)}) %copy-start) | copy-done | bytes 65560
  6.8 0.0 copy-start.2
  6.8 0.8 %copy-done.2 = bf16[128,256]{1,0:T(8,128)(2,1)S(1)} copy-done((bf16[128,256]{1,0:T(8,128)(2,1)S(1)}, bf16[128,256]{1,0:T(8,128)(2,1)}, u32[]{:S(2)}) %copy-start.2) | copy-done | bytes 65560
  7.7 0.0 copy-start.1
  7.7 0.0 copy-start.3
  7.7 1.1 %own_share.1 = (f32[16,256]{1,0:T(8,128)S(1)}, s32[2,128]{1,0:T(2,128)S(1)}) custom-call(s32[2]{0:T(128)S(1)} %add_add_fusion.place_ref, bf16[1,2048]{1,0:T(2,128)(2,1)S(1)} %copy-done.4, bf16[128,256]{1,0:T(8,128)(2,1)S(1)} %copy-done, bf16[128,256]{1,0:T(8,128)(2,1)S(1)} %copy-done.2, s32[1,128]{1,0:T(1,128)S(1)} %bitcast.6, ...), custom_call_target="tpu_custom_call" | custom-call | flops 4194304 | bytes 524288 | tf_op jit(solution)/shard_map/own_share/pallas_call | solution.py:152
  8.8 0.0 collective-permute-done.4.query_ref
  8.8 0.0 copy-done.1
  8.8 0.0 copy-done.3
  8.8 0.6 %other_share.1 = f32[16,256]{1,0:T(8,128)S(1)} custom-call(bf16[1,2048]{1,0:T(2,128)(2,1)S(1)} %collective-permute-done.4.query_ref, s32[2,128]{1,0:T(2,128)S(1)} %get-tuple-element.5.shown_ref, bf16[128,256]{1,0:T(8,128)(2,1)S(1)} %copy-done.1, bf16[128,256]{1,0:T(8,128)(2,1)S(1)} %copy-done.3, bf16[128,256]{1,0:T(8,128)(2,1)S(1)} %collective-permute-done.refs_3_.refs_2_, ...), custom_call_target="tpu_custom_call" | custom-call | flops 4194304 | bytes 524288 | tf_op jit(solution)/shard_map/other_share/pallas_call | solution.py:165
  9.5 0.3 %collective-permute-start.6 = (f32[16,256]{1,0:T(8,128)S(1)}, f32[16,256]{1,0:T(8,128)S(1)}, u32[]{:S(2)}, u32[]{:S(2)}) collective-permute-start(f32[16,256]{1,0:T(8,128)S(1)} %other_share.1), channel_id=1, source_target_pairs={{0,16},{4,20},{8,24},{12,28},{16,0},{20,4},{24,8},{28,12},{1,17},{... | collective-permute-start | bytes 49160 | tf_op jit(solution)/shard_map/ppermute | solution.py:145
  9.7 2.7 %collective-permute-start.5 = (f32[16,256]{1,0:T(8,128)S(1)}, f32[16,256]{1,0:T(8,128)S(1)}, u32[]{:S(2)}, u32[]{:S(2)}) collective-permute-start(f32[16,256]{1,0:T(8,128)S(1)} %other_share.1), channel_id=1, source_target_pairs={{0,20},{4,16},{8,28},{12,24},{16,4},{20,0},{24,12},{28,8},{1,21},{... | collective-permute-start | bytes 49160 | tf_op jit(solution)/shard_map/ppermute | solution.py:145
  12.4 0.5 %collective-permute-start.3 = (f32[16,256]{1,0:T(8,128)S(1)}, f32[16,256]{1,0:T(8,128)S(1)}, u32[]{:S(2)}, u32[]{:S(2)}) collective-permute-start(f32[16,256]{1,0:T(8,128)S(1)} %get-tuple-element.4.refs_0_), channel_id=1, source_target_pairs={{0,4},{4,0},{8,12},{12,8},{16,20},{20,16},{24,28},{28,24},{1,5},{5... | collective-permute-start | bytes 49160 | tf_op jit(solution)/shard_map/ppermute | solution.py:145
  13.0 0.2 %collective-permute-done.6.refs_3_ = f32[16,256]{1,0:T(8,128)S(1)} collective-permute-done((f32[16,256]{1,0:T(8,128)S(1)}, f32[16,256]{1,0:T(8,128)S(1)}, u32[]{:S(2)}, u32[]{:S(2)}) %collective-permute-start.6) | collective-permute-done | bytes 16416 | tf_op jit(solution)/shard_map/ppermute | solution.py:145
  13.2 1.2 %collective-permute-done.5.refs_2_ = f32[16,256]{1,0:T(8,128)S(1)} collective-permute-done((f32[16,256]{1,0:T(8,128)S(1)}, f32[16,256]{1,0:T(8,128)S(1)}, u32[]{:S(2)}, u32[]{:S(2)}) %collective-permute-start.5) | collective-permute-done | bytes 16416 | tf_op jit(solution)/shard_map/ppermute | solution.py:145
  14.4 1.8 %collective-permute-done.3.refs_1_ = f32[16,256]{1,0:T(8,128)S(1)} collective-permute-done((f32[16,256]{1,0:T(8,128)S(1)}, f32[16,256]{1,0:T(8,128)S(1)}, u32[]{:S(2)}, u32[]{:S(2)}) %collective-permute-start.3) | collective-permute-done | bytes 16416 | tf_op jit(solution)/shard_map/ppermute | solution.py:145
  16.2 0.8 %combine.1 = (bf16[1,2048]{1,0:T(2,128)(2,1)}, f32[1,16]{1,0:T(1,128)}) custom-call(f32[16,256]{1,0:T(8,128)S(1)} %get-tuple-element.4.refs_0_, f32[16,256]{1,0:T(8,128)S(1)} %collective-permute-done.3.refs_1_, f32[16,256]{1,0:T(8,128)S(1)} %collective-permute-done.5.refs_2_, f32[16,256]{1,0:T(8,128)S(1)} %collective-permute-done.6.refs_3_), custom_call_target="tpu_custom_call" | custom-call | flops 65536 | bytes 8192 | tf_op jit(solution)/shard_map/combine/pallas_call | solution.py:121
Async XLA Ops:
  0.6 0.7 %copy-start.5 = (s32[128]{0:T(128)S(1)}, s32[128]{0:T(128)}, u32[]{:S(2)}) copy-start(s32[128]{0:T(128)} %param.8) | copy-start | bytes 1540
  1.3 4.3 %collective-permute-start.2 = (s32[1,128]{1,0:T(1,128)S(1)}, s32[1,128]{1,0:T(1,128)S(1)}, u32[]{:S(2)}, u32[]{:S(2)}) collective-permute-start(s32[1,128]{1,0:T(1,128)S(1)} %bitcast.5), channel_id=1, source_target_pairs={{0,8},{4,12},{8,0},{12,4},{16,24},{20,28},{24,16},{28,20},{1,9},{5... | collective-permute-start | bytes 1544 | tf_op jit(solution)/shard_map/ppermute | solution.py:145
  1.8 7.0 %collective-permute-start.4 = (bf16[1,2048]{1,0:T(2,128)(2,1)}, bf16[1,2048]{1,0:T(2,128)(2,1)S(1)}, u32[]{:S(2)}, u32[]{:S(2)}) collective-permute-start(bf16[1,2048]{1,0:T(2,128)(2,1)} %query_ref.1), channel_id=1, source_target_pairs={{0,16},{4,20},{8,24},{12,28},{16,0},{20,4},{24,8},{28,12},{1,17},{... | collective-permute-start | bytes 12296 | tf_op jit(solution)/shard_map/ppermute | solution.py:145
  4.3 1.5 %collective-permute-start = (bf16[128,256]{1,0:T(8,128)(2,1)}, bf16[128,256]{1,0:T(8,128)(2,1)S(1)}, u32[]{:S(2)}, u32[]{:S(2)}) collective-permute-start(bf16[128,256]{1,0:T(8,128)(2,1)} %refs_0_.3), channel_id=1, source_target_pairs={{0,8},{4,12},{8,0},{12,4},{16,24},{20,28},{24,16},{28,20},{1,9},{5... | collective-permute-start | bytes 196616 | tf_op jit(solution)/shard_map/ppermute | solution.py:145
  4.5 1.5 %collective-permute-start.1 = (bf16[128,256]{1,0:T(8,128)(2,1)}, bf16[128,256]{1,0:T(8,128)(2,1)S(1)}, u32[]{:S(2)}, u32[]{:S(2)}) collective-permute-start(bf16[128,256]{1,0:T(8,128)(2,1)} %refs_1_.3), channel_id=1, source_target_pairs={{0,8},{4,12},{8,0},{12,4},{16,24},{20,28},{24,16},{28,20},{1,9},{5... | collective-permute-start | bytes 196616 | tf_op jit(solution)/shard_map/ppermute | solution.py:145
  4.8 1.2 %copy-start.4 = (bf16[1,2048]{1,0:T(2,128)(2,1)S(1)}, bf16[1,2048]{1,0:T(2,128)(2,1)}, u32[]{:S(2)}) copy-start(bf16[1,2048]{1,0:T(2,128)(2,1)} %query_ref.1) | copy-start | bytes 12292
  6.0 0.8 %copy-start = (bf16[128,256]{1,0:T(8,128)(2,1)S(1)}, bf16[128,256]{1,0:T(8,128)(2,1)}, u32[]{:S(2)}) copy-start(bf16[128,256]{1,0:T(8,128)(2,1)} %refs_0_.3) | copy-start | bytes 196612
  6.8 0.8 %copy-start.2 = (bf16[128,256]{1,0:T(8,128)(2,1)S(1)}, bf16[128,256]{1,0:T(8,128)(2,1)}, u32[]{:S(2)}) copy-start(bf16[128,256]{1,0:T(8,128)(2,1)} %refs_1_.3) | copy-start | bytes 196612
  7.7 1.2 %copy-start.1 = (bf16[128,256]{1,0:T(8,128)(2,1)S(1)}, bf16[128,256]{1,0:T(8,128)(2,1)}, u32[]{:S(2)}) copy-start(bf16[128,256]{1,0:T(8,128)(2,1)} %refs_0_.3) | copy-start | bytes 196612
  7.7 1.2 %copy-start.3 = (bf16[128,256]{1,0:T(8,128)(2,1)S(1)}, bf16[128,256]{1,0:T(8,128)(2,1)}, u32[]{:S(2)}) copy-start(bf16[128,256]{1,0:T(8,128)(2,1)} %refs_1_.3) | copy-start | bytes 196612
  9.5 3.8 %collective-permute-start.6 = (f32[16,256]{1,0:T(8,128)S(1)}, f32[16,256]{1,0:T(8,128)S(1)}, u32[]{:S(2)}, u32[]{:S(2)}) collective-permute-start(f32[16,256]{1,0:T(8,128)S(1)} %other_share.1), channel_id=1, source_target_pairs={{0,16},{4,20},{8,24},{12,28},{16,0},{20,4},{24,8},{28,12},{1,17},{... | collective-permute-start | bytes 49160 | tf_op jit(solution)/shard_map/ppermute | solution.py:145
  9.7 4.6 %collective-permute-start.5 = (f32[16,256]{1,0:T(8,128)S(1)}, f32[16,256]{1,0:T(8,128)S(1)}, u32[]{:S(2)}, u32[]{:S(2)}) collective-permute-start(f32[16,256]{1,0:T(8,128)S(1)} %other_share.1), channel_id=1, source_target_pairs={{0,20},{4,16},{8,28},{12,24},{16,4},{20,0},{24,12},{28,8},{1,21},{... | collective-permute-start | bytes 49160 | tf_op jit(solution)/shard_map/ppermute | solution.py:145
  12.4 3.7 %collective-permute-start.3 = (f32[16,256]{1,0:T(8,128)S(1)}, f32[16,256]{1,0:T(8,128)S(1)}, u32[]{:S(2)}, u32[]{:S(2)}) collective-permute-start(f32[16,256]{1,0:T(8,128)S(1)} %get-tuple-element.4.refs_0_), channel_id=1, source_target_pairs={{0,4},{4,0},{8,12},{12,8},{16,20},{20,16},{24,28},{28,24},{1,5},{5... | collective-permute-start | bytes 49160 | tf_op jit(solution)/shard_map/ppermute | solution.py:145

commit v2 on v1

--- a/solution.py
+++ b/solution.py
@@ -8,9 +8,9 @@
 from jax.experimental.pallas import tpu as pltpu
 from jax.sharding import PartitionSpec as P
 
+
 HD = 128
 HIDDEN = -1e30
-DIRECT_DEVICES = 16
 VMEM_BYTES = 8 * 1024 * 1024
 
 
@@ -77,21 +77,17 @@
     return jnp.concatenate(packed, axis=0)
 
 
-def first_kernel(place_ref, query_ref, *refs):
-    n = (len(refs) - 2) // 3
+def clock_kernel(owners, start_ref, clock_ref):
+    for i, owner in enumerate(owners):
+        at = start_ref[0] + owner(lax.axis_index("blk"))
+        clock_ref[i : i + 1] = jnp.full((1, clock_ref.shape[1]), at, jnp.int32)
+
+
+def share_kernel(row, clock_ref, query_ref, *refs):
+    n = (len(refs) - 1) // 3
     blocks = [(refs[3 * i][...], refs[3 * i + 1][...]) for i in range(n)]
-    rows = [refs[3 * i + 2][...] for i in range(n)]
-    share_ref, shown_ref = refs[-2:]
-    own, other = place_ref[0], place_ref[1]
-    share_ref[...] = share_of(query_ref[...], blocks, [r <= own for r in rows])
-    for i, r in enumerate(rows):
-        shown_ref[i : i + 1] = (r <= other).astype(jnp.int32)
-
-
-def second_kernel(query_ref, shown_ref, *refs):
-    n = (len(refs) - 1) // 2
-    blocks = [(refs[2 * i][...], refs[2 * i + 1][...]) for i in range(n)]
-    shown = [shown_ref[i : i + 1] > 0 for i in range(n)]
+    clock = clock_ref[row : row + 1]
+    shown = [refs[3 * i + 2][...] <= clock for i in range(n)]
     refs[-1][...] = share_of(query_ref[...], blocks, shown)
 
 
@@ -144,34 +140,32 @@
         ]
         return lax.ppermute(value, both, pairs)
 
-    owner = lax.axis_index("blk")
+    def share(row, query):
+        return pl.pallas_call(
+            functools.partial(share_kernel, row),
+            out_shape=whole((heads, 2 * HD), jnp.float32),
+            in_specs=in_vmem(8),
+            out_specs=in_vmem(1)[0],
+            compiler_params=params(),
+            cost_estimate=cost(1 << 22),
+        )(clock, query, cache_keys, cache_values, places, *far)
+
     places = cache_places[None, :]
-    other_query = swap(queries, 2, 0)
-    far = [swap(x, 1, 0) for x in (cache_keys, cache_values, places)]
-    at = span_start[0] + jnp.stack([owner, owner ^ 2]).astype(jnp.int32)
-    own_share, shown = pl.pallas_call(
-        first_kernel,
-        out_shape=(
-            whole((heads, 2 * HD), jnp.float32),
-            whole((2, row_count), jnp.int32),
-        ),
-        in_specs=[pl.BlockSpec(memory_space=pltpu.SMEM)] + in_vmem(7),
-        out_specs=tuple(in_vmem(2)),
-        compiler_params=params(),
-        cost_estimate=cost(1 << 22),
-        name="own_share",
-    )(at, queries, cache_keys, cache_values, places, *far)
-    shares = [own_share, swap(own_share, 0, 1)]
-    other_share = pl.pallas_call(
-        second_kernel,
-        out_shape=whole((heads, 2 * HD), jnp.float32),
-        in_specs=in_vmem(6),
+    other_query = swap(queries, 3, 0)
+    far = [swap(cache_keys, 1, 0), swap(cache_values, 1, 0), swap(places, 1, 0)]
+    clock = pl.pallas_call(
+        functools.partial(clock_kernel, (lambda b: b, lambda b: b ^ 3)),
+        out_shape=whole((2, row_count), jnp.int32),
+        in_specs=[pl.BlockSpec(memory_space=pltpu.SMEM)],
         out_specs=in_vmem(1)[0],
         compiler_params=params(),
-        cost_estimate=cost(1 << 22),
-        name="other_share",
-    )(other_query, shown, cache_keys, cache_values, *far[:2])
-    shares += [swap(other_share, 2, 1), swap(other_share, 2, 0)]
+        cost_estimate=pl.CostEstimate(flops=1 << 27, bytes_accessed=4096, transcendentals=0),
+        name="clock",
+    )(span_start)
+    own_share = share(0, queries)
+    across = swap(own_share, 0, 1)
+    other_share = share(1, other_query)
+    shares = [own_share, across, swap(other_share, 3, 1), swap(other_share, 3, 0)]
     return combine(shares, columns)
 
 
@@ -222,9 +216,10 @@
         P(),
     )
     blk, sub = mesh.shape["blk"], mesh.shape["sub"]
+    is_direct = (blk, sub) == (4, 2) and mesh.size <= 32
 
     def on_device(queries, *cache):
-        if (blk, sub) == (4, 2) and queries.shape[0] == 1:
+        if is_direct and queries.shape[0] == 1:
             return direct((blk, sub), queries, *cache)
         return grouped(queries, *cache)
 

time: 17.2 us -> 13.8 us (0.80)
  the two profiles are of different devices: /device:TPU:0 before, /device:TPU:1 now
where the time goes in v2:
time: 13.8 us; the launch traced here: 13.6 us
  starting transfers between devices  6.16 us (45%)
  waiting for transfers between devices  3.25 us (24%)
  Pallas kernels  2 us (14%)
  between operations  1.35 us (10%)
  local copies, waits for them, and re-layouts  0.87 us (6%)
    ppermute x7, starting transfers between devices, swap(): return lax.ppermute(value, both, pairs)  6.16 us
    ppermute x7, waiting for transfers between devices, swap(): return lax.ppermute(value, both, pairs)  3.25 us
    pallas_call x2, Pallas kernels, share(): pl.pallas_call(functools.partial(share_kernel, row), out_shape=whole((hea...  1.22 us
    unnamed x8, local copies, waits for them, and re-layouts  0.87 us
    pallas_call x1, Pallas kernels, combine(): pl.pallas_call(combine_kernel, out_shape=(whole((1, columns), jnp.bfloat1...  0.77 us
  transfers between devices with their start and end apart: 7, of which 2 were waited for; matrix products, arithmetic and copies ran while one was open for 0% of the time, Pallas kernels for 9%

profile of v2, /device:TPU:1, one launch (start us, length us, event | category | flops | bytes accessed | tf_op | source)
XLA Modules:
  0.0 13.6 jit_solution(13609360103407459020)
XLA Ops:
  0.6 0.0 copy-start.3
  0.6 0.1 collective-permute-start
  0.7 0.5 %collective-permute-start.1 = (bf16[128,256]{1,0:T(8,128)(2,1)}, bf16[128,256]{1,0:T(8,128)(2,1)S(1)}, u32[]{:S(2)}, u32[]{:S(2)}) collective-permute-start(bf16[128,256]{1,0:T(8,128)(2,1)} %refs_1_.3), channel_id=1, source_target_pairs={{0,8},{4,12},{8,0},{12,4},{16,24},{20,28},{24,16},{28,20},{1,9},{5... | collective-permute-start | bytes 196616 | tf_op jit(solution)/shard_map/ppermute | solution.py:141
  1.2 0.1 copy-done.3
  1.3 0.0 collective-permute-start.2
  1.3 2.6 %collective-permute-start.4 = (bf16[1,2048]{1,0:T(2,128)(2,1)}, bf16[1,2048]{1,0:T(2,128)(2,1)S(1)}, u32[]{:S(2)}, u32[]{:S(2)}) collective-permute-start(bf16[1,2048]{1,0:T(2,128)(2,1)} %query_ref.1), channel_id=1, source_target_pairs={{0,24},{4,28},{8,16},{12,20},{16,8},{20,12},{24,0},{28,4},{1,25},{... | collective-permute-start | bytes 12296 | tf_op jit(solution)/shard_map/ppermute | solution.py:141
  4.6 0.0 copy-start
  4.6 0.0 copy-start.1
  4.6 0.0 copy-start.2
  4.6 0.0 collective-permute-done.2.refs_5_
  4.6 0.0 collective-permute-done.refs_3_
  4.6 0.0 collective-permute-done.1.refs_4_
  4.6 0.8 %copy-done = bf16[128,256]{1,0:T(8,128)(2,1)S(1)} copy-done((bf16[128,256]{1,0:T(8,128)(2,1)S(1)}, bf16[128,256]{1,0:T(8,128)(2,1)}, u32[]{:S(2)}) %copy-start) | copy-done | bytes 65560
  5.4 0.0 copy-done.1
  5.4 0.0 copy-done.2
  5.4 0.6 %shard_map.68.refs_0_ = f32[16,256]{1,0:T(8,128)S(1)} custom-call(s32[2,128]{1,0:T(2,128)S(1)} %clock.1.clock_ref, bf16[1,2048]{1,0:T(2,128)(2,1)S(1)} %copy-done.2, bf16[128,256]{1,0:T(8,128)(2,1)S(1)} %copy-done, bf16[128,256]{1,0:T(8,128)(2,1)S(1)} %copy-done.1, s32[1,128]{1,0:T(1,128)S(1)} %bitcast.2, bf16[128,256]{1,0:T(8,128)(2,1)S(1)} %collective-permute-done.refs_3_, ...), custom_call_target="tpu_custom_call" | custom-call | flops 4194304 | bytes 524288 | tf_op jit(solution)/shard_map/pallas_call | solution.py:144
  6.1 1.2 %collective-permute-start.3 = (f32[16,256]{1,0:T(8,128)S(1)}, f32[16,256]{1,0:T(8,128)S(1)}, u32[]{:S(2)}, u32[]{:S(2)}) collective-permute-start(f32[16,256]{1,0:T(8,128)S(1)} %shard_map.68.refs_0_), channel_id=1, source_target_pairs={{0,4},{4,0},{8,12},{12,8},{16,20},{20,16},{24,28},{28,24},{1,5},{5... | collective-permute-start | bytes 49160 | tf_op jit(solution)/shard_map/ppermute | solution.py:141
  7.3 0.0 collective-permute-done.4.query_ref
  7.3 0.6 %shard_map.69 = f32[16,256]{1,0:T(8,128)S(1)} custom-call(s32[2,128]{1,0:T(2,128)S(1)} %clock.1.clock_ref, bf16[1,2048]{1,0:T(2,128)(2,1)S(1)} %collective-permute-done.4.query_ref, bf16[128,256]{1,0:T(8,128)(2,1)S(1)} %copy-done, bf16[128,256]{1,0:T(8,128)(2,1)S(1)} %copy-done.1, s32[1,128]{1,0:T(1,128)S(1)} %bitcast.3, ...), custom_call_target="tpu_custom_call" | custom-call | flops 4194304 | bytes 524288 | tf_op jit(solution)/shard_map/pallas_call | solution.py:144
  7.9 0.9 %collective-permute-start.6 = (f32[16,256]{1,0:T(8,128)S(1)}, f32[16,256]{1,0:T(8,128)S(1)}, u32[]{:S(2)}, u32[]{:S(2)}) collective-permute-start(f32[16,256]{1,0:T(8,128)S(1)} %shard_map.69), channel_id=1, source_target_pairs={{0,24},{4,28},{8,16},{12,20},{16,8},{20,12},{24,0},{28,4},{1,25},{... | collective-permute-start | bytes 49160 | tf_op jit(solution)/shard_map/ppermute | solution.py:141
  8.8 0.8 %collective-permute-start.5 = (f32[16,256]{1,0:T(8,128)S(1)}, f32[16,256]{1,0:T(8,128)S(1)}, u32[]{:S(2)}, u32[]{:S(2)}) collective-permute-start(f32[16,256]{1,0:T(8,128)S(1)} %shard_map.69), channel_id=1, source_target_pairs={{0,28},{4,24},{8,20},{12,16},{16,12},{20,8},{24,4},{28,0},{1,29},{... | collective-permute-start | bytes 49160 | tf_op jit(solution)/shard_map/ppermute | solution.py:141
  9.6 0.0 collective-permute-done.3.refs_1_
  9.6 1.8 %collective-permute-done.6.refs_3_ = f32[16,256]{1,0:T(8,128)S(1)} collective-permute-done((f32[16,256]{1,0:T(8,128)S(1)}, f32[16,256]{1,0:T(8,128)S(1)}, u32[]{:S(2)}, u32[]{:S(2)}) %collective-permute-start.6) | collective-permute-done | bytes 16416 | tf_op jit(solution)/shard_map/ppermute | solution.py:141
  11.4 1.4 %collective-permute-done.5.refs_2_ = f32[16,256]{1,0:T(8,128)S(1)} collective-permute-done((f32[16,256]{1,0:T(8,128)S(1)}, f32[16,256]{1,0:T(8,128)S(1)}, u32[]{:S(2)}, u32[]{:S(2)}) %collective-permute-start.5) | collective-permute-done | bytes 16416 | tf_op jit(solution)/shard_map/ppermute | solution.py:141
  12.9 0.8 %combine.1 = (bf16[1,2048]{1,0:T(2,128)(2,1)}, f32[1,16]{1,0:T(1,128)}) custom-call(f32[16,256]{1,0:T(8,128)S(1)} %shard_map.68.refs_0_, f32[16,256]{1,0:T(8,128)S(1)} %collective-permute-done.3.refs_1_, f32[16,256]{1,0:T(8,128)S(1)} %collective-permute-done.5.refs_2_, f32[16,256]{1,0:T(8,128)S(1)} %collective-permute-done.6.refs_3_), custom_call_target="tpu_custom_call" | custom-call | flops 65536 | bytes 8192 | tf_op jit(solution)/shard_map/combine/pallas_call | solution.py:117
  (1 shorter events, 0.0 us)
Async XLA Ops:
  0.6 0.7 %copy-start.3 = (s32[128]{0:T(128)S(1)}, s32[128]{0:T(128)}, u32[]{:S(2)}) copy-start(s32[128]{0:T(128)} %param.8) | copy-start | bytes 1540
  0.6 4.0 %collective-permute-start = (bf16[128,256]{1,0:T(8,128)(2,1)}, bf16[128,256]{1,0:T(8,128)(2,1)S(1)}, u32[]{:S(2)}, u32[]{:S(2)}) collective-permute-start(bf16[128,256]{1,0:T(8,128)(2,1)} %refs_0_.3), channel_id=1, source_target_pairs={{0,8},{4,12},{8,0},{12,4},{16,24},{20,28},{24,16},{28,20},{1,9},{5... | collective-permute-start | bytes 196616 | tf_op jit(solution)/shard_map/ppermute | solution.py:141
  0.7 3.9 %collective-permute-start.1 = (bf16[128,256]{1,0:T(8,128)(2,1)}, bf16[128,256]{1,0:T(8,128)(2,1)S(1)}, u32[]{:S(2)}, u32[]{:S(2)}) collective-permute-start(bf16[128,256]{1,0:T(8,128)(2,1)} %refs_1_.3), channel_id=1, source_target_pairs={{0,8},{4,12},{8,0},{12,4},{16,24},{20,28},{24,16},{28,20},{1,9},{5... | collective-permute-start | bytes 196616 | tf_op jit(solution)/shard_map/ppermute | solution.py:141
  1.3 3.3 %collective-permute-start.2 = (s32[1,128]{1,0:T(1,128)S(1)}, s32[1,128]{1,0:T(1,128)S(1)}, u32[]{:S(2)}, u32[]{:S(2)}) collective-permute-start(s32[1,128]{1,0:T(1,128)S(1)} %bitcast.1), channel_id=1, source_target_pairs={{0,8},{4,12},{8,0},{12,4},{16,24},{20,28},{24,16},{28,20},{1,9},{5... | collective-permute-start | bytes 1544 | tf_op jit(solution)/shard_map/ppermute | solution.py:141
  1.3 6.0 %collective-permute-start.4 = (bf16[1,2048]{1,0:T(2,128)(2,1)}, bf16[1,2048]{1,0:T(2,128)(2,1)S(1)}, u32[]{:S(2)}, u32[]{:S(2)}) collective-permute-start(bf16[1,2048]{1,0:T(2,128)(2,1)} %query_ref.1), channel_id=1, source_target_pairs={{0,24},{4,28},{8,16},{12,20},{16,8},{20,12},{24,0},{28,4},{1,25},{... | collective-permute-start | bytes 12296 | tf_op jit(solution)/shard_map/ppermute | solution.py:141
  4.6 0.8 %copy-start = (bf16[128,256]{1,0:T(8,128)(2,1)S(1)}, bf16[128,256]{1,0:T(8,128)(2,1)}, u32[]{:S(2)}) copy-start(bf16[128,256]{1,0:T(8,128)(2,1)} %refs_0_.3) | copy-start | bytes 196612
  4.6 0.9 %copy-start.1 = (bf16[128,256]{1,0:T(8,128)(2,1)S(1)}, bf16[128,256]{1,0:T(8,128)(2,1)}, u32[]{:S(2)}) copy-start(bf16[128,256]{1,0:T(8,128)(2,1)} %refs_1_.3) | copy-start | bytes 196612
  4.6 0.9 %copy-start.2 = (bf16[1,2048]{1,0:T(2,128)(2,1)S(1)}, bf16[1,2048]{1,0:T(2,128)(2,1)}, u32[]{:S(2)}) copy-start(bf16[1,2048]{1,0:T(2,128)(2,1)} %query_ref.1) | copy-start | bytes 12292
  6.1 3.6 %collective-permute-start.3 = (f32[16,256]{1,0:T(8,128)S(1)}, f32[16,256]{1,0:T(8,128)S(1)}, u32[]{:S(2)}, u32[]{:S(2)}) collective-permute-start(f32[16,256]{1,0:T(8,128)S(1)} %shard_map.68.refs_0_), channel_id=1, source_target_pairs={{0,4},{4,0},{8,12},{12,8},{16,20},{20,16},{24,28},{28,24},{1,5},{5... | collective-permute-start | bytes 49160 | tf_op jit(solution)/shard_map/ppermute | solution.py:141
  7.9 3.6 %collective-permute-start.6 = (f32[16,256]{1,0:T(8,128)S(1)}, f32[16,256]{1,0:T(8,128)S(1)}, u32[]{:S(2)}, u32[]{:S(2)}) collective-permute-start(f32[16,256]{1,0:T(8,128)S(1)} %shard_map.69), channel_id=1, source_target_pairs={{0,24},{4,28},{8,16},{12,20},{16,8},{20,12},{24,0},{28,4},{1,25},{... | collective-permute-start | bytes 49160 | tf_op jit(solution)/shard_map/ppermute | solution.py:141
  8.8 4.1 %collective-permute-start.5 = (f32[16,256]{1,0:T(8,128)S(1)}, f32[16,256]{1,0:T(8,128)S(1)}, u32[]{:S(2)}, u32[]{:S(2)}) collective-permute-start(f32[16,256]{1,0:T(8,128)S(1)} %shard_map.69), channel_id=1, source_target_pairs={{0,28},{4,24},{8,20},{12,16},{16,12},{20,8},{24,4},{28,0},{1,29},{... | collective-permute-start | bytes 49160 | tf_op jit(solution)/shard_map/ppermute | solution.py:141

commit v3 on v2

--- a/solution.py
+++ b/solution.py
@@ -77,10 +77,14 @@
     return jnp.concatenate(packed, axis=0)
 
 
-def clock_kernel(owners, start_ref, clock_ref):
+def tokens_kernel(owners, tokens_ref):
     for i, owner in enumerate(owners):
-        at = start_ref[0] + owner(lax.axis_index("blk"))
-        clock_ref[i : i + 1] = jnp.full((1, clock_ref.shape[1]), at, jnp.int32)
+        at = owner(lax.axis_index("blk"))
+        tokens_ref[i : i + 1] = jnp.full((1, tokens_ref.shape[1]), at, jnp.int32)
+
+
+def clock_kernel(start_ref, tokens_ref, clock_ref):
+    clock_ref[...] = tokens_ref[...] + start_ref[0]
 
 
 def share_kernel(row, clock_ref, query_ref, *refs):
@@ -153,15 +157,25 @@
     places = cache_places[None, :]
     other_query = swap(queries, 3, 0)
     far = [swap(cache_keys, 1, 0), swap(cache_values, 1, 0), swap(places, 1, 0)]
-    clock = pl.pallas_call(
-        functools.partial(clock_kernel, (lambda b: b, lambda b: b ^ 3)),
+    tokens = pl.pallas_call(
+        functools.partial(tokens_kernel, (lambda b: b, lambda b: b ^ 3)),
         out_shape=whole((2, row_count), jnp.int32),
-        in_specs=[pl.BlockSpec(memory_space=pltpu.SMEM)],
         out_specs=in_vmem(1)[0],
         compiler_params=params(),
-        cost_estimate=pl.CostEstimate(flops=1 << 27, bytes_accessed=4096, transcendentals=0),
+        cost_estimate=pl.CostEstimate(
+            flops=1 << 27, bytes_accessed=4096, transcendentals=0
+        ),
+        name="tokens",
+    )()
+    clock = pl.pallas_call(
+        clock_kernel,
+        out_shape=whole((2, row_count), jnp.int32),
+        in_specs=[pl.BlockSpec(memory_space=pltpu.SMEM)] + in_vmem(1),
+        out_specs=in_vmem(1)[0],
+        compiler_params=params(),
+        cost_estimate=cost(1 << 12),
         name="clock",
-    )(span_start)
+    )(span_start, tokens)
     own_share = share(0, queries)
     across = swap(own_share, 0, 1)
     other_share = share(1, other_query)

time: 13.8 us -> 13.3 us (0.964)
  the two profiles are of different devices: /device:TPU:1 before, /device:TPU:0 now
where the time goes in v3:
time: 13.3 us; the launch traced here: 13.1 us
  starting transfers between devices  6.98 us (52%)
  waiting for transfers between devices  2.78 us (21%)
  Pallas kernels  2 us (15%)
  between operations  1.37 us (10%)
    ppermute x7, starting transfers between devices, swap(): return lax.ppermute(value, both, pairs)  6.98 us
    ppermute x7, waiting for transfers between devices, swap(): return lax.ppermute(value, both, pairs)  2.78 us
    pallas_call x2, Pallas kernels, share(): pl.pallas_call(functools.partial(share_kernel, row), out_shape=whole((hea...  1.22 us
    pallas_call x1, Pallas kernels, combine(): pl.pallas_call(combine_kernel, out_shape=(whole((1, columns), jnp.bfloat1...  0.77 us
  transfers between devices with their start and end apart: 7, of which 2 were waited for; matrix products, arithmetic and copies ran while one was open for 0% of the time, Pallas kernels for 9%

profile of v3, /device:TPU:0, one launch (start us, length us, event | category | flops | bytes accessed | tf_op | source)
XLA Modules:
  0.0 13.1 jit_solution(2219177800144038874)
XLA Ops:
  0.6 0.0 copy-start.3
  0.6 0.6 %collective-permute-start = (bf16[128,256]{1,0:T(8,128)(2,1)}, bf16[128,256]{1,0:T(8,128)(2,1)S(1)}, u32[]{:S(2)}, u32[]{:S(2)}) collective-permute-start(bf16[128,256]{1,0:T(8,128)(2,1)} %refs_0_.3), channel_id=1, source_target_pairs={{0,8},{4,12},{8,0},{12,4},{16,24},{20,28},{24,16},{28,20},{1,9},{5... | collective-permute-start | bytes 196616 | tf_op jit(solution)/shard_map/ppermute | solution.py:145
  1.2 0.1 collective-permute-start.1
  1.3 0.0 copy-done.3
  1.3 0.0 copy-start
  1.3 0.0 copy-start.1
  1.3 0.5 %collective-permute-start.2 = (s32[1,128]{1,0:T(1,128)S(1)}, s32[1,128]{1,0:T(1,128)S(1)}, u32[]{:S(2)}, u32[]{:S(2)}) collective-permute-start(s32[1,128]{1,0:T(1,128)S(1)} %bitcast.1), channel_id=1, source_target_pairs={{0,8},{4,12},{8,0},{12,4},{16,24},{20,28},{24,16},{28,20},{1,9},{5... | collective-permute-start | bytes 1544 | tf_op jit(solution)/shard_map/ppermute | solution.py:145
  1.8 2.6 %collective-permute-start.4 = (bf16[1,2048]{1,0:T(2,128)(2,1)}, bf16[1,2048]{1,0:T(2,128)(2,1)S(1)}, u32[]{:S(2)}, u32[]{:S(2)}) collective-permute-start(bf16[1,2048]{1,0:T(2,128)(2,1)} %query_ref.1), channel_id=1, source_target_pairs={{0,24},{4,28},{8,16},{12,20},{16,8},{20,12},{24,0},{28,4},{1,25},{... | collective-permute-start | bytes 12296 | tf_op jit(solution)/shard_map/ppermute | solution.py:145
  4.4 0.0 copy-start.2
  5.1 0.0 collective-permute-done.2.refs_5_
  5.1 0.0 collective-permute-done.refs_3_
  5.1 0.0 collective-permute-done.1.refs_4_
  5.1 0.0 copy-done
  5.1 0.0 copy-done.1
  5.1 0.0 copy-done.2
  5.1 0.6 %shard_map.68.refs_0_ = f32[16,256]{1,0:T(8,128)S(1)} custom-call(s32[2,128]{1,0:T(2,128)S(1)} %clock.1.clock_ref, bf16[1,2048]{1,0:T(2,128)(2,1)S(1)} %copy-done.2, bf16[128,256]{1,0:T(8,128)(2,1)S(1)} %copy-done, bf16[128,256]{1,0:T(8,128)(2,1)S(1)} %copy-done.1, s32[1,128]{1,0:T(1,128)S(1)} %bitcast.2, bf16[128,256]{1,0:T(8,128)(2,1)S(1)} %collective-permute-done.refs_3_, ...), custom_call_target="tpu_custom_call" | custom-call | flops 4194304 | bytes 524288 | tf_op jit(solution)/shard_map/pallas_call | solution.py:148
  5.8 1.5 %collective-permute-start.3 = (f32[16,256]{1,0:T(8,128)S(1)}, f32[16,256]{1,0:T(8,128)S(1)}, u32[]{:S(2)}, u32[]{:S(2)}) collective-permute-start(f32[16,256]{1,0:T(8,128)S(1)} %shard_map.68.refs_0_), channel_id=1, source_target_pairs={{0,4},{4,0},{8,12},{12,8},{16,20},{20,16},{24,28},{28,24},{1,5},{5... | collective-permute-start | bytes 49160 | tf_op jit(solution)/shard_map/ppermute | solution.py:145
  7.3 0.0 collective-permute-done.4.query_ref
  7.3 0.6 %shard_map.69 = f32[16,256]{1,0:T(8,128)S(1)} custom-call(s32[2,128]{1,0:T(2,128)S(1)} %clock.1.clock_ref, bf16[1,2048]{1,0:T(2,128)(2,1)S(1)} %collective-permute-done.4.query_ref, bf16[128,256]{1,0:T(8,128)(2,1)S(1)} %copy-done, bf16[128,256]{1,0:T(8,128)(2,1)S(1)} %copy-done.1, s32[1,128]{1,0:T(1,128)S(1)} %bitcast.3, ...), custom_call_target="tpu_custom_call" | custom-call | flops 4194304 | bytes 524288 | tf_op jit(solution)/shard_map/pallas_call | solution.py:148
  7.9 0.4 %collective-permute-start.6 = (f32[16,256]{1,0:T(8,128)S(1)}, f32[16,256]{1,0:T(8,128)S(1)}, u32[]{:S(2)}, u32[]{:S(2)}) collective-permute-start(f32[16,256]{1,0:T(8,128)S(1)} %shard_map.69), channel_id=1, source_target_pairs={{0,24},{4,28},{8,16},{12,20},{16,8},{20,12},{24,0},{28,4},{1,25},{... | collective-permute-start | bytes 49160 | tf_op jit(solution)/shard_map/ppermute | solution.py:145
  8.3 1.3 %collective-permute-start.5 = (f32[16,256]{1,0:T(8,128)S(1)}, f32[16,256]{1,0:T(8,128)S(1)}, u32[]{:S(2)}, u32[]{:S(2)}) collective-permute-start(f32[16,256]{1,0:T(8,128)S(1)} %shard_map.69), channel_id=1, source_target_pairs={{0,28},{4,24},{8,20},{12,16},{16,12},{20,8},{24,4},{28,0},{1,29},{... | collective-permute-start | bytes 49160 | tf_op jit(solution)/shard_map/ppermute | solution.py:145
  9.6 0.0 collective-permute-done.3.refs_1_
  9.6 1.6 %collective-permute-done.6.refs_3_ = f32[16,256]{1,0:T(8,128)S(1)} collective-permute-done((f32[16,256]{1,0:T(8,128)S(1)}, f32[16,256]{1,0:T(8,128)S(1)}, u32[]{:S(2)}, u32[]{:S(2)}) %collective-permute-start.6) | collective-permute-done | bytes 16416 | tf_op jit(solution)/shard_map/ppermute | solution.py:145
  11.2 1.2 %collective-permute-done.5.refs_2_ = f32[16,256]{1,0:T(8,128)S(1)} collective-permute-done((f32[16,256]{1,0:T(8,128)S(1)}, f32[16,256]{1,0:T(8,128)S(1)}, u32[]{:S(2)}, u32[]{:S(2)}) %collective-permute-start.5) | collective-permute-done | bytes 16416 | tf_op jit(solution)/shard_map/ppermute | solution.py:145
  12.4 0.8 %combine.1 = (bf16[1,2048]{1,0:T(2,128)(2,1)}, f32[1,16]{1,0:T(1,128)}) custom-call(f32[16,256]{1,0:T(8,128)S(1)} %shard_map.68.refs_0_, f32[16,256]{1,0:T(8,128)S(1)} %collective-permute-done.3.refs_1_, f32[16,256]{1,0:T(8,128)S(1)} %collective-permute-done.5.refs_2_, f32[16,256]{1,0:T(8,128)S(1)} %collective-permute-done.6.refs_3_), custom_call_target="tpu_custom_call" | custom-call | flops 65536 | bytes 8192 | tf_op jit(solution)/shard_map/combine/pallas_call | solution.py:121
  (2 shorter events, 0.0 us)
Async XLA Ops:
  0.6 0.7 %copy-start.3 = (s32[128]{0:T(128)S(1)}, s32[128]{0:T(128)}, u32[]{:S(2)}) copy-start(s32[128]{0:T(128)} %param.8) | copy-start | bytes 1540
  0.6 4.5 %collective-permute-start = (bf16[128,256]{1,0:T(8,128)(2,1)}, bf16[128,256]{1,0:T(8,128)(2,1)S(1)}, u32[]{:S(2)}, u32[]{:S(2)}) collective-permute-start(bf16[128,256]{1,0:T(8,128)(2,1)} %refs_0_.3), channel_id=1, source_target_pairs={{0,8},{4,12},{8,0},{12,4},{16,24},{20,28},{24,16},{28,20},{1,9},{5... | collective-permute-start | bytes 196616 | tf_op jit(solution)/shard_map/ppermute | solution.py:145
  1.2 3.9 %collective-permute-start.1 = (bf16[128,256]{1,0:T(8,128)(2,1)}, bf16[128,256]{1,0:T(8,128)(2,1)S(1)}, u32[]{:S(2)}, u32[]{:S(2)}) collective-permute-start(bf16[128,256]{1,0:T(8,128)(2,1)} %refs_1_.3), channel_id=1, source_target_pairs={{0,8},{4,12},{8,0},{12,4},{16,24},{20,28},{24,16},{28,20},{1,9},{5... | collective-permute-start | bytes 196616 | tf_op jit(solution)/shard_map/ppermute | solution.py:145
  1.3 3.8 %copy-start = (bf16[128,256]{1,0:T(8,128)(2,1)S(1)}, bf16[128,256]{1,0:T(8,128)(2,1)}, u32[]{:S(2)}) copy-start(bf16[128,256]{1,0:T(8,128)(2,1)} %refs_0_.3) | copy-start | bytes 196612
  1.3 3.8 %copy-start.1 = (bf16[128,256]{1,0:T(8,128)(2,1)S(1)}, bf16[128,256]{1,0:T(8,128)(2,1)}, u32[]{:S(2)}) copy-start(bf16[128,256]{1,0:T(8,128)(2,1)} %refs_1_.3) | copy-start | bytes 196612
  1.3 3.8 %collective-permute-start.2 = (s32[1,128]{1,0:T(1,128)S(1)}, s32[1,128]{1,0:T(1,128)S(1)}, u32[]{:S(2)}, u32[]{:S(2)}) collective-permute-start(s32[1,128]{1,0:T(1,128)S(1)} %bitcast.1), channel_id=1, source_target_pairs={{0,8},{4,12},{8,0},{12,4},{16,24},{20,28},{24,16},{28,20},{1,9},{5... | collective-permute-start | bytes 1544 | tf_op jit(solution)/shard_map/ppermute | solution.py:145
  1.8 5.5 %collective-permute-start.4 = (bf16[1,2048]{1,0:T(2,128)(2,1)}, bf16[1,2048]{1,0:T(2,128)(2,1)S(1)}, u32[]{:S(2)}, u32[]{:S(2)}) collective-permute-start(bf16[1,2048]{1,0:T(2,128)(2,1)} %query_ref.1), channel_id=1, source_target_pairs={{0,24},{4,28},{8,16},{12,20},{16,8},{20,12},{24,0},{28,4},{1,25},{... | collective-permute-start | bytes 12296 | tf_op jit(solution)/shard_map/ppermute | solution.py:145
  4.4 0.7 %copy-start.2 = (bf16[1,2048]{1,0:T(2,128)(2,1)S(1)}, bf16[1,2048]{1,0:T(2,128)(2,1)}, u32[]{:S(2)}) copy-start(bf16[1,2048]{1,0:T(2,128)(2,1)} %query_ref.1) | copy-start | bytes 12292
  5.8 3.9 %collective-permute-start.3 = (f32[16,256]{1,0:T(8,128)S(1)}, f32[16,256]{1,0:T(8,128)S(1)}, u32[]{:S(2)}, u32[]{:S(2)}) collective-permute-start(f32[16,256]{1,0:T(8,128)S(1)} %shard_map.68.refs_0_), channel_id=1, source_target_pairs={{0,4},{4,0},{8,12},{12,8},{16,20},{20,16},{24,28},{28,24},{1,5},{5... | collective-permute-start | bytes 49160 | tf_op jit(solution)/shard_map/ppermute | solution.py:145
  7.9 3.3 %collective-permute-start.6 = (f32[16,256]{1,0:T(8,128)S(1)}, f32[16,256]{1,0:T(8,128)S(1)}, u32[]{:S(2)}, u32[]{:S(2)}) collective-permute-start(f32[16,256]{1,0:T(8,128)S(1)} %shard_map.69), channel_id=1, source_target_pairs={{0,24},{4,28},{8,16},{12,20},{16,8},{20,12},{24,0},{28,4},{1,25},{... | collective-permute-start | bytes 49160 | tf_op jit(solution)/shard_map/ppermute | solution.py:145
  8.3 4.1 %collective-permute-start.5 = (f32[16,256]{1,0:T(8,128)S(1)}, f32[16,256]{1,0:T(8,128)S(1)}, u32[]{:S(2)}, u32[]{:S(2)}) collective-permute-start(f32[16,256]{1,0:T(8,128)S(1)} %shard_map.69), channel_id=1, source_target_pairs={{0,28},{4,24},{8,20},{12,16},{16,12},{20,8},{24,4},{28,0},{1,29},{... | collective-permute-start | bytes 49160 | tf_op jit(solution)/shard_map/ppermute | solution.py:145

commit v4 on v3

--- a/solution.py
+++ b/solution.py
@@ -34,47 +34,37 @@
     heads = query.shape[1] // HD
     kv_heads = blocks[0][0].shape[1] // HD
     group = heads // kv_heads
-    lane = lax.broadcasted_iota(jnp.int32, (group, HD), 1)
-    packed = []
-    for j in range(kv_heads):
-        first = j * group
-        q = jnp.concatenate(
-            [query[:, (first + i) * HD : (first + i + 1) * HD] for i in range(group)], axis=0
+    rows = jnp.concatenate([query[:, i * HD : (i + 1) * HD] for i in range(heads)], axis=0)
+    kv_of = lax.broadcasted_iota(jnp.int32, (heads, HD), 0) // group
+    lane = lax.broadcasted_iota(jnp.int32, (heads, HD), 1)
+    spread = jnp.concatenate(
+        [jnp.where(kv_of == j, rows, jnp.zeros_like(rows)) for j in range(kv_heads)], axis=1
+    )
+    scores = [
+        jnp.where(
+            shown,
+            lax.dot_general(
+                spread, keys, (((1,), (1,)), ((), ())), preferred_element_type=jnp.float32
+            )
+            * (1.0 / math.sqrt(HD)),
+            HIDDEN,
         )
-        scores = [
-            jnp.where(
-                shown,
-                lax.dot_general(
-                    q,
-                    keys[:, j * HD : (j + 1) * HD],
-                    (((1,), (1,)), ((), ())),
-                    preferred_element_type=jnp.float32,
-                )
-                * (1.0 / math.sqrt(HD)),
-                HIDDEN,
-            )
-            for (keys, _), shown in zip(blocks, shown_rows, strict=True)
-        ]
-        peak = functools.reduce(
-            jnp.maximum, [jnp.max(s, axis=1, keepdims=True) for s in scores]
-        )
-        weights = [
-            jnp.where(shown, jnp.exp(s - peak), 0.0).astype(jnp.bfloat16)
-            for s, shown in zip(scores, shown_rows, strict=True)
-        ]
-        denominator = sum(
-            jnp.sum(w.astype(jnp.float32), axis=1, keepdims=True) for w in weights
-        )
-        numerator = sum(
-            jnp.dot(w, values[:, j * HD : (j + 1) * HD], preferred_element_type=jnp.float32)
-            for w, (_, values) in zip(weights, blocks, strict=True)
-        )
-        packed.append(
-            jnp.concatenate(
-                [numerator, jnp.where(lane < HD // 2, peak, denominator)], axis=1
-            )
-        )
-    return jnp.concatenate(packed, axis=0)
+        for (keys, _), shown in zip(blocks, shown_rows, strict=True)
+    ]
+    peak = functools.reduce(jnp.maximum, [jnp.max(s, axis=1, keepdims=True) for s in scores])
+    weights = [
+        jnp.where(shown, jnp.exp(s - peak), 0.0).astype(jnp.bfloat16)
+        for s, shown in zip(scores, shown_rows, strict=True)
+    ]
+    denominator = sum(jnp.sum(w.astype(jnp.float32), axis=1, keepdims=True) for w in weights)
+    wide = sum(
+        jnp.dot(w, values, preferred_element_type=jnp.float32)
+        for w, (_, values) in zip(weights, blocks, strict=True)
+    )
+    numerator = wide[:, :HD]
+    for j in range(1, kv_heads):
+        numerator = jnp.where(kv_of == j, wide[:, j * HD : (j + 1) * HD], numerator)
+    return jnp.concatenate([numerator, jnp.where(lane < HD // 2, peak, denominator)], axis=1)
 
 
 def tokens_kernel(owners, tokens_ref):

time: 13.3 us -> 13.1 us (0.985)
  Pallas kernels: 2 us -> 1.46 us
  waiting for transfers between devices: 2.78 us -> 2.99 us
    pallas_call x2, Pallas kernels: 1.22 us -> 0.69 us  [share(): pl.pallas_call(functools.partial(share_kernel, row), out_shape=whole((hea...]
    ppermute x7, waiting for transfers between devices: 2.78 us -> 2.99 us  [swap(): return lax.ppermute(value, both, pairs)]
  transfers between devices with their start and end apart: 7 -> 7, of which waited for: 2 -> 3; matrix products, arithmetic and copies ran while one was open for 0% -> 0% of each run, Pallas kernels for 9% -> 5%
where the time goes in v4:
time: 13.1 us; the launch traced here: 12.9 us
  starting transfers between devices  7.04 us (54%)
  waiting for transfers between devices  2.99 us (23%)
  Pallas kernels  1.46 us (11%)
  between operations  1.37 us (10%)
    ppermute x7, starting transfers between devices, swap(): return lax.ppermute(value, both, pairs)  7.04 us
    ppermute x7, waiting for transfers between devices, swap(): return lax.ppermute(value, both, pairs)  2.99 us
    pallas_call x1, Pallas kernels, combine(): pl.pallas_call(combine_kernel, out_shape=(whole((1, columns), jnp.bfloat1...  0.77 us
    pallas_call x2, Pallas kernels, share(): pl.pallas_call(functools.partial(share_kernel, row), out_shape=whole((hea...  0.69 us
  transfers between devices with their start and end apart: 7, of which 3 were waited for; matrix products, arithmetic and copies ran while one was open for 0% of the time, Pallas kernels for 5%

profile of v4, /device:TPU:0, one launch (start us, length us, event | category | flops | bytes accessed | tf_op | source)
XLA Modules:
  0.0 12.9 jit_solution(12417099230993808546)
XLA Ops:
  0.6 0.0 copy-start.3
  0.6 0.6 %collective-permute-start = (bf16[128,256]{1,0:T(8,128)(2,1)}, bf16[128,256]{1,0:T(8,128)(2,1)S(1)}, u32[]{:S(2)}, u32[]{:S(2)}) collective-permute-start(bf16[128,256]{1,0:T(8,128)(2,1)} %refs_0_.3), channel_id=1, source_target_pairs={{0,8},{4,12},{8,0},{12,4},{16,24},{20,28},{24,16},{28,20},{1,9},{5... | collective-permute-start | bytes 196616 | tf_op jit(solution)/shard_map/ppermute | solution.py:135
  1.2 0.1 collective-permute-start.1
  1.3 0.0 copy-done.3
  1.3 0.0 copy-start
  1.3 0.0 copy-start.1
  1.3 0.5 %collective-permute-start.2 = (s32[1,128]{1,0:T(1,128)S(1)}, s32[1,128]{1,0:T(1,128)S(1)}, u32[]{:S(2)}, u32[]{:S(2)}) collective-permute-start(s32[1,128]{1,0:T(1,128)S(1)} %bitcast.1), channel_id=1, source_target_pairs={{0,8},{4,12},{8,0},{12,4},{16,24},{20,28},{24,16},{28,20},{1,9},{5... | collective-permute-start | bytes 1544 | tf_op jit(solution)/shard_map/ppermute | solution.py:135
  1.8 2.6 %collective-permute-start.4 = (bf16[1,2048]{1,0:T(2,128)(2,1)}, bf16[1,2048]{1,0:T(2,128)(2,1)S(1)}, u32[]{:S(2)}, u32[]{:S(2)}) collective-permute-start(bf16[1,2048]{1,0:T(2,128)(2,1)} %query_ref.1), channel_id=1, source_target_pairs={{0,24},{4,28},{8,16},{12,20},{16,8},{20,12},{24,0},{28,4},{1,25},{... | collective-permute-start | bytes 12296 | tf_op jit(solution)/shard_map/ppermute | solution.py:135
  4.4 0.0 copy-start.2
  5.1 0.0 collective-permute-done.2.refs_5_
  5.1 0.0 collective-permute-done.refs_3_
  5.1 0.0 collective-permute-done.1.refs_4_
  5.1 0.0 copy-done
  5.1 0.0 copy-done.1
  5.1 0.0 copy-done.2
  5.1 0.3 %shard_map.68.refs_0_ = f32[16,256]{1,0:T(8,128)S(1)} custom-call(s32[2,128]{1,0:T(2,128)S(1)} %clock.1.clock_ref, bf16[1,2048]{1,0:T(2,128)(2,1)S(1)} %copy-done.2, bf16[128,256]{1,0:T(8,128)(2,1)S(1)} %copy-done, bf16[128,256]{1,0:T(8,128)(2,1)S(1)} %copy-done.1, s32[1,128]{1,0:T(1,128)S(1)} %bitcast.2, bf16[128,256]{1,0:T(8,128)(2,1)S(1)} %collective-permute-done.refs_3_, ...), custom_call_target="tpu_custom_call" | custom-call | flops 4194304 | bytes 524288 | tf_op jit(solution)/shard_map/pallas_call | solution.py:138
  5.5 1.5 %collective-permute-start.3 = (f32[16,256]{1,0:T(8,128)S(1)}, f32[16,256]{1,0:T(8,128)S(1)}, u32[]{:S(2)}, u32[]{:S(2)}) collective-permute-start(f32[16,256]{1,0:T(8,128)S(1)} %shard_map.68.refs_0_), channel_id=1, source_target_pairs={{0,4},{4,0},{8,12},{12,8},{16,20},{20,16},{24,28},{28,24},{1,5},{5... | collective-permute-start | bytes 49160 | tf_op jit(solution)/shard_map/ppermute | solution.py:135
  7.0 0.0 collective-permute-done.4.query_ref
  7.0 0.3 %shard_map.69 = f32[16,256]{1,0:T(8,128)S(1)} custom-call(s32[2,128]{1,0:T(2,128)S(1)} %clock.1.clock_ref, bf16[1,2048]{1,0:T(2,128)(2,1)S(1)} %collective-permute-done.4.query_ref, bf16[128,256]{1,0:T(8,128)(2,1)S(1)} %copy-done, bf16[128,256]{1,0:T(8,128)(2,1)S(1)} %copy-done.1, s32[1,128]{1,0:T(1,128)S(1)} %bitcast.3, ...), custom_call_target="tpu_custom_call" | custom-call | flops 4194304 | bytes 524288 | tf_op jit(solution)/shard_map/pallas_call | solution.py:138
  7.3 0.7 %collective-permute-start.6 = (f32[16,256]{1,0:T(8,128)S(1)}, f32[16,256]{1,0:T(8,128)S(1)}, u32[]{:S(2)}, u32[]{:S(2)}) collective-permute-start(f32[16,256]{1,0:T(8,128)S(1)} %shard_map.69), channel_id=1, source_target_pairs={{0,24},{4,28},{8,16},{12,20},{16,8},{20,12},{24,0},{28,4},{1,25},{... | collective-permute-start | bytes 49160 | tf_op jit(solution)/shard_map/ppermute | solution.py:135
  8.0 1.1 %collective-permute-start.5 = (f32[16,256]{1,0:T(8,128)S(1)}, f32[16,256]{1,0:T(8,128)S(1)}, u32[]{:S(2)}, u32[]{:S(2)}) collective-permute-start(f32[16,256]{1,0:T(8,128)S(1)} %shard_map.69), channel_id=1, source_target_pairs={{0,28},{4,24},{8,20},{12,16},{16,12},{20,8},{24,4},{28,0},{1,29},{... | collective-permute-start | bytes 49160 | tf_op jit(solution)/shard_map/ppermute | solution.py:135
  9.1 0.1 collective-permute-done.3.refs_1_
  9.2 1.4 %collective-permute-done.6.refs_3_ = f32[16,256]{1,0:T(8,128)S(1)} collective-permute-done((f32[16,256]{1,0:T(8,128)S(1)}, f32[16,256]{1,0:T(8,128)S(1)}, u32[]{:S(2)}, u32[]{:S(2)}) %collective-permute-start.6) | collective-permute-done | bytes 16416 | tf_op jit(solution)/shard_map/ppermute | solution.py:135
  10.6 1.5 %collective-permute-done.5.refs_2_ = f32[16,256]{1,0:T(8,128)S(1)} collective-permute-done((f32[16,256]{1,0:T(8,128)S(1)}, f32[16,256]{1,0:T(8,128)S(1)}, u32[]{:S(2)}, u32[]{:S(2)}) %collective-permute-start.5) | collective-permute-done | bytes 16416 | tf_op jit(solution)/shard_map/ppermute | solution.py:135
  12.1 0.8 %combine.1 = (bf16[1,2048]{1,0:T(2,128)(2,1)}, f32[1,16]{1,0:T(1,128)}) custom-call(f32[16,256]{1,0:T(8,128)S(1)} %shard_map.68.refs_0_, f32[16,256]{1,0:T(8,128)S(1)} %collective-permute-done.3.refs_1_, f32[16,256]{1,0:T(8,128)S(1)} %collective-permute-done.5.refs_2_, f32[16,256]{1,0:T(8,128)S(1)} %collective-permute-done.6.refs_3_), custom_call_target="tpu_custom_call" | custom-call | flops 65536 | bytes 8192 | tf_op jit(solution)/shard_map/combine/pallas_call | solution.py:111
  (2 shorter events, 0.0 us)
Async XLA Ops:
  0.6 0.7 %copy-start.3 = (s32[128]{0:T(128)S(1)}, s32[128]{0:T(128)}, u32[]{:S(2)}) copy-start(s32[128]{0:T(128)} %param.8) | copy-start | bytes 1540
  0.6 4.5 %collective-permute-start = (bf16[128,256]{1,0:T(8,128)(2,1)}, bf16[128,256]{1,0:T(8,128)(2,1)S(1)}, u32[]{:S(2)}, u32[]{:S(2)}) collective-permute-start(bf16[128,256]{1,0:T(8,128)(2,1)} %refs_0_.3), channel_id=1, source_target_pairs={{0,8},{4,12},{8,0},{12,4},{16,24},{20,28},{24,16},{28,20},{1,9},{5... | collective-permute-start | bytes 196616 | tf_op jit(solution)/shard_map/ppermute | solution.py:135
  1.2 3.9 %collective-permute-start.1 = (bf16[128,256]{1,0:T(8,128)(2,1)}, bf16[128,256]{1,0:T(8,128)(2,1)S(1)}, u32[]{:S(2)}, u32[]{:S(2)}) collective-permute-start(bf16[128,256]{1,0:T(8,128)(2,1)} %refs_1_.3), channel_id=1, source_target_pairs={{0,8},{4,12},{8,0},{12,4},{16,24},{20,28},{24,16},{28,20},{1,9},{5... | collective-permute-start | bytes 196616 | tf_op jit(solution)/shard_map/ppermute | solution.py:135
  1.3 3.8 %copy-start = (bf16[128,256]{1,0:T(8,128)(2,1)S(1)}, bf16[128,256]{1,0:T(8,128)(2,1)}, u32[]{:S(2)}) copy-start(bf16[128,256]{1,0:T(8,128)(2,1)} %refs_0_.3) | copy-start | bytes 196612
  1.3 3.8 %copy-start.1 = (bf16[128,256]{1,0:T(8,128)(2,1)S(1)}, bf16[128,256]{1,0:T(8,128)(2,1)}, u32[]{:S(2)}) copy-start(bf16[128,256]{1,0:T(8,128)(2,1)} %refs_1_.3) | copy-start | bytes 196612
  1.3 3.8 %collective-permute-start.2 = (s32[1,128]{1,0:T(1,128)S(1)}, s32[1,128]{1,0:T(1,128)S(1)}, u32[]{:S(2)}, u32[]{:S(2)}) collective-permute-start(s32[1,128]{1,0:T(1,128)S(1)} %bitcast.1), channel_id=1, source_target_pairs={{0,8},{4,12},{8,0},{12,4},{16,24},{20,28},{24,16},{28,20},{1,9},{5... | collective-permute-start | bytes 1544 | tf_op jit(solution)/shard_map/ppermute | solution.py:135
  1.8 5.2 %collective-permute-start.4 = (bf16[1,2048]{1,0:T(2,128)(2,1)}, bf16[1,2048]{1,0:T(2,128)(2,1)S(1)}, u32[]{:S(2)}, u32[]{:S(2)}) collective-permute-start(bf16[1,2048]{1,0:T(2,128)(2,1)} %query_ref.1), channel_id=1, source_target_pairs={{0,24},{4,28},{8,16},{12,20},{16,8},{20,12},{24,0},{28,4},{1,25},{... | collective-permute-start | bytes 12296 | tf_op jit(solution)/shard_map/ppermute | solution.py:135
  4.4 0.7 %copy-start.2 = (bf16[1,2048]{1,0:T(2,128)(2,1)S(1)}, bf16[1,2048]{1,0:T(2,128)(2,1)}, u32[]{:S(2)}) copy-start(bf16[1,2048]{1,0:T(2,128)(2,1)} %query_ref.1) | copy-start | bytes 12292
  5.5 3.8 %collective-permute-start.3 = (f32[16,256]{1,0:T(8,128)S(1)}, f32[16,256]{1,0:T(8,128)S(1)}, u32[]{:S(2)}, u32[]{:S(2)}) collective-permute-start(f32[16,256]{1,0:T(8,128)S(1)} %shard_map.68.refs_0_), channel_id=1, source_target_pairs={{0,4},{4,0},{8,12},{12,8},{16,20},{20,16},{24,28},{28,24},{1,5},{5... | collective-permute-start | bytes 49160 | tf_op jit(solution)/shard_map/ppermute | solution.py:135
  7.3 3.3 %collective-permute-start.6 = (f32[16,256]{1,0:T(8,128)S(1)}, f32[16,256]{1,0:T(8,128)S(1)}, u32[]{:S(2)}, u32[]{:S(2)}) collective-permute-start(f32[16,256]{1,0:T(8,128)S(1)} %shard_map.69), channel_id=1, source_target_pairs={{0,24},{4,28},{8,16},{12,20},{16,8},{20,12},{24,0},{28,4},{1,25},{... | collective-permute-start | bytes 49160 | tf_op jit(solution)/shard_map/ppermute | solution.py:135
  8.0 4.1 %collective-permute-start.5 = (f32[16,256]{1,0:T(8,128)S(1)}, f32[16,256]{1,0:T(8,128)S(1)}, u32[]{:S(2)}, u32[]{:S(2)}) collective-permute-start(f32[16,256]{1,0:T(8,128)S(1)} %shard_map.69), channel_id=1, source_target_pairs={{0,28},{4,24},{8,20},{12,16},{16,12},{20,8},{24,4},{28,0},{1,29},{... | collective-permute-start | bytes 49160 | tf_op jit(solution)/shard_map/ppermute | solution.py:135

commit v5 on v4

--- a/solution.py
+++ b/solution.py
@@ -11,6 +11,8 @@
 
 HD = 128
 HIDDEN = -1e30
+DIGIT_ROWS = 16
+STRETCH = 16
 VMEM_BYTES = 8 * 1024 * 1024
 
 
@@ -28,6 +30,15 @@
 
 def cost(flops):
     return pl.CostEstimate(flops=flops, bytes_accessed=flops // 8, transcendentals=0)
+
+
+def terms_of(column):
+    terms = []
+    for _ in range(3):
+        term = column.astype(jnp.bfloat16).astype(jnp.float32)
+        terms.append(term)
+        column = column - term
+    return terms
 
 
 def share_of(query, blocks, shown_rows):
@@ -64,7 +75,11 @@
     numerator = wide[:, :HD]
     for j in range(1, kv_heads):
         numerator = jnp.where(kv_of == j, wide[:, j * HD : (j + 1) * HD], numerator)
-    return jnp.concatenate([numerator, jnp.where(lane < HD // 2, peak, denominator)], axis=1)
+    terms = [*terms_of(peak), *terms_of(denominator)]
+    stats = terms[-1]
+    for i in range(len(terms) - 2, -1, -1):
+        stats = jnp.where(lane < (i + 1) * STRETCH, terms[i], stats)
+    return jnp.concatenate([numerator, stats], axis=1).astype(jnp.bfloat16)
 
 
 def tokens_kernel(owners, tokens_ref):
@@ -77,25 +92,43 @@
     clock_ref[...] = tokens_ref[...] + start_ref[0]
 
 
+def pack_kernel(keys_ref, values_ref, places_ref, packed_ref):
+    rows, columns = keys_ref.shape
+    packed_ref[:rows] = keys_ref[...]
+    packed_ref[rows : 2 * rows] = values_ref[...]
+    places = places_ref[...].reshape(1, rows)
+    digit = lax.broadcasted_iota(jnp.int32, (DIGIT_ROWS, rows), 0)
+    digits = jnp.where(digit == 0, places >> 8, jnp.where(digit == 1, places & 255, 0))
+    packed_ref[2 * rows :, :rows] = digits.astype(jnp.float32).astype(jnp.bfloat16)
+    packed_ref[2 * rows :, rows:] = jnp.zeros((DIGIT_ROWS, columns - rows), jnp.bfloat16)
+
+
 def share_kernel(row, clock_ref, query_ref, *refs):
-    n = (len(refs) - 1) // 3
-    blocks = [(refs[3 * i][...], refs[3 * i + 1][...]) for i in range(n)]
-    clock = clock_ref[row : row + 1]
-    shown = [refs[3 * i + 2][...] <= clock for i in range(n)]
+    clock = clock_ref[row : row + 1].astype(jnp.float32)
+    rows = (refs[0].shape[0] - DIGIT_ROWS) // 2
+    blocks, shown = [], []
+    for ref in refs[:-1]:
+        blocks.append((ref[:rows], ref[rows : 2 * rows]))
+        digits = ref[2 * rows :, :rows].astype(jnp.float32)
+        shown.append(digits[:1] * 256.0 + digits[1:2] <= clock)
     refs[-1][...] = share_of(query_ref[...], blocks, shown)
 
 
+def stat_of(share, first):
+    at = HD + first * STRETCH
+    terms = [share[:, at + i * STRETCH : at + i * STRETCH + 1] for i in range(3)]
+    return terms[0] + terms[1] + terms[2]
+
+
 def combine_kernel(*refs):
-    shares = [r[...] for r in refs[:-2]]
+    shares = [r[...].astype(jnp.float32) for r in refs[:-2]]
     out_ref, peak_ref = refs[-2:]
     heads = shares[0].shape[0]
-    peaks = [s[:, HD : HD + 1] for s in shares]
+    peaks = [stat_of(s, 0) for s in shares]
     peak = functools.reduce(jnp.maximum, peaks)
     scales = [jnp.exp(p - peak) for p in peaks]
     numerator = sum(s[:, :HD] * c for s, c in zip(shares, scales, strict=True))
-    denominator = sum(
-        s[:, HD + HD // 2 : HD + HD // 2 + 1] * c for s, c in zip(shares, scales, strict=True)
-    )
+    denominator = sum(stat_of(s, 3) * c for s, c in zip(shares, scales, strict=True))
     out = (numerator / denominator).astype(jnp.bfloat16)
     for h in range(heads):
         out_ref[:, h * HD : (h + 1) * HD] = out[h : h + 1]
@@ -137,16 +170,24 @@
     def share(row, query):
         return pl.pallas_call(
             functools.partial(share_kernel, row),
-            out_shape=whole((heads, 2 * HD), jnp.float32),
-            in_specs=in_vmem(8),
+            out_shape=whole((heads, 2 * HD), jnp.bfloat16),
+            in_specs=in_vmem(4),
             out_specs=in_vmem(1)[0],
             compiler_params=params(),
             cost_estimate=cost(1 << 22),
-        )(clock, query, cache_keys, cache_values, places, *far)
-
-    places = cache_places[None, :]
+        )(clock, query, mine, theirs)
+
     other_query = swap(queries, 3, 0)
-    far = [swap(cache_keys, 1, 0), swap(cache_values, 1, 0), swap(places, 1, 0)]
+    mine = pl.pallas_call(
+        pack_kernel,
+        out_shape=whole((2 * row_count + DIGIT_ROWS, cache_keys.shape[1]), jnp.bfloat16),
+        in_specs=in_vmem(3),
+        out_specs=in_vmem(1)[0],
+        compiler_params=params(),
+        cost_estimate=cost(1 << 12),
+        name="pack",
+    )(cache_keys, cache_values, cache_places)
+    theirs = swap(mine, 1, 0)
     tokens = pl.pallas_call(
         functools.partial(tokens_kernel, (lambda b: b, lambda b: b ^ 3)),
         out_shape=whole((2, row_count), jnp.int32),

time: 13.1 us -> 15 us (1.15)
  local copies, waits for them, and re-layouts: 0.02 us -> 2.45 us
  waiting for transfers between devices: 2.99 us -> 2.55 us
  starting transfers between devices: 7.04 us -> 6.82 us
    unnamed x8, local copies, waits for them, and re-layouts: 0.02 us -> 2.45 us
    ppermute x7 -> x5, waiting for transfers between devices: 2.99 us -> 2.55 us  [swap(): return lax.ppermute(value, both, pairs)]
    ppermute x7 -> x5, starting transfers between devices: 7.04 us -> 6.82 us  [swap(): return lax.ppermute(value, both, pairs)]
  transfers between devices with their start and end apart: 7 -> 5, of which waited for: 3 -> 2; matrix products, arithmetic and copies ran while one was open for 0% -> 0% of each run, Pallas kernels for 5% -> 5%
where the time goes in v5:
time: 15 us; the launch traced here: 14.7 us
  starting transfers between devices  6.82 us (45%)
  waiting for transfers between devices  2.55 us (17%)
  local copies, waits for them, and re-layouts  2.45 us (16%)
  Pallas kernels  1.57 us (10%)
  between operations  1.32 us (9%)
    ppermute x5, starting transfers between devices, swap(): return lax.ppermute(value, both, pairs)  6.82 us
    ppermute x5, waiting for transfers between devices, swap(): return lax.ppermute(value, both, pairs)  2.55 us
    unnamed x8, local copies, waits for them, and re-layouts  2.45 us
    pallas_call x1, Pallas kernels, combine(): pl.pallas_call(combine_kernel, out_shape=(whole((1, columns), jnp.bfloat1...  0.85 us
    pallas_call x2, Pallas kernels, share(): pl.pallas_call(functools.partial(share_kernel, row), out_shape=whole((hea...  0.7 us
  transfers between devices with their start and end apart: 5, of which 2 were waited for; matrix products, arithmetic and copies ran while one was open for 0% of the time, Pallas kernels for 5%

profile of v5, /device:TPU:0, one launch (start us, length us, event | category | flops | bytes accessed | tf_op | source)
XLA Modules:
  0.0 14.7 jit_solution(554129878857979616)
XLA Ops:
  0.6 0.0 copy-start
  0.6 0.8 %copy-done = bf16[128,256]{1,0:T(8,128)(2,1)S(1)} copy-done((bf16[128,256]{1,0:T(8,128)(2,1)S(1)}, bf16[128,256]{1,0:T(8,128)(2,1)}, u32[]{:S(2)}) %copy-start) | copy-done | bytes 65560
  1.5 0.0 copy-start.1
  1.5 0.8 %copy-done.1 = bf16[128,256]{1,0:T(8,128)(2,1)S(1)} copy-done((bf16[128,256]{1,0:T(8,128)(2,1)S(1)}, bf16[128,256]{1,0:T(8,128)(2,1)}, u32[]{:S(2)}) %copy-start.1) | copy-done | bytes 65560
  2.3 0.0 copy-start.3
  2.3 0.7 %copy-done.3 = s32[128]{0:T(128)S(1)} copy-done((s32[128]{0:T(128)S(1)}, s32[128]{0:T(128)}, u32[]{:S(2)}) %copy-start.3) | copy-done | bytes 536
  3.0 0.0 copy-start.2
  3.0 0.6 %collective-permute-start = (bf16[272,256]{1,0:T(8,128)(2,1)S(1)}, bf16[272,256]{1,0:T(8,128)(2,1)S(1)}, u32[]{:S(2)}, u32[]{:S(2)}) collective-permute-start(bf16[272,256]{1,0:T(8,128)(2,1)S(1)} %pack.1.refs_0_), channel_id=1, source_target_pairs={{0,8},{4,12},{8,0},{12,4},{16,24},{20,28},{24,16},{28,20},{1,9},{5... | collective-permute-start | bytes 417800 | tf_op jit(solution)/shard_map/ppermute | solution.py:168
  3.5 0.1 copy-done.2
  3.7 2.5 %collective-permute-start.2 = (bf16[1,2048]{1,0:T(2,128)(2,1)S(1)}, bf16[1,2048]{1,0:T(2,128)(2,1)S(1)}, u32[]{:S(2)}, u32[]{:S(2)}) collective-permute-start(bf16[1,2048]{1,0:T(2,128)(2,1)S(1)} %copy-done.2), channel_id=1, source_target_pairs={{0,24},{4,28},{8,16},{12,20},{16,8},{20,12},{24,0},{28,4},{1,25},{... | collective-permute-start | bytes 12296 | tf_op jit(solution)/shard_map/ppermute | solution.py:168
  6.8 0.0 collective-permute-done.refs_1_
  6.8 0.3 %shard_map.68.refs_0_ = bf16[16,256]{1,0:T(8,128)(2,1)S(1)} custom-call(s32[2,128]{1,0:T(2,128)S(1)} %clock.1.clock_ref, bf16[1,2048]{1,0:T(2,128)(2,1)S(1)} %copy-done.2, bf16[272,256]{1,0:T(8,128)(2,1)S(1)} %pack.1.refs_0_, bf16[272,256]{1,0:T(8,128)(2,1)S(1)} %collective-permute-done.refs_1_), custom_call_target="tpu_custom_call" | custom-call | flops 4194304 | bytes 524288 | tf_op jit(solution)/shard_map/pallas_call | solution.py:171
  7.2 1.5 %collective-permute-start.1 = (bf16[16,256]{1,0:T(8,128)(2,1)S(1)}, bf16[16,256]{1,0:T(8,128)(2,1)S(1)}, u32[]{:S(2)}, u32[]{:S(2)}) collective-permute-start(bf16[16,256]{1,0:T(8,128)(2,1)S(1)} %shard_map.68.refs_0_), channel_id=1, source_target_pairs={{0,4},{4,0},{8,12},{12,8},{16,20},{20,16},{24,28},{28,24},{1,5},{5... | collective-permute-start | bytes 24584 | tf_op jit(solution)/shard_map/ppermute | solution.py:168
  8.7 0.0 collective-permute-done.2.query_ref
  8.7 0.3 %shard_map.69 = bf16[16,256]{1,0:T(8,128)(2,1)S(1)} custom-call(s32[2,128]{1,0:T(2,128)S(1)} %clock.1.clock_ref, bf16[1,2048]{1,0:T(2,128)(2,1)S(1)} %collective-permute-done.2.query_ref, bf16[272,256]{1,0:T(8,128)(2,1)S(1)} %pack.1.refs_0_, bf16[272,256]{1,0:T(8,128)(2,1)S(1)} %collective-permute-done.refs_1_), custom_call_target="tpu_custom_call" | custom-call | flops 4194304 | bytes 524288 | tf_op jit(solution)/shard_map/pallas_call | solution.py:171
  9.1 0.8 %collective-permute-start.4 = (bf16[16,256]{1,0:T(8,128)(2,1)S(1)}, bf16[16,256]{1,0:T(8,128)(2,1)S(1)}, u32[]{:S(2)}, u32[]{:S(2)}) collective-permute-start(bf16[16,256]{1,0:T(8,128)(2,1)S(1)} %shard_map.69), channel_id=1, source_target_pairs={{0,24},{4,28},{8,16},{12,20},{16,8},{20,12},{24,0},{28,4},{1,25},{... | collective-permute-start | bytes 24584 | tf_op jit(solution)/shard_map/ppermute | solution.py:168
  9.9 1.4 %collective-permute-start.3 = (bf16[16,256]{1,0:T(8,128)(2,1)S(1)}, bf16[16,256]{1,0:T(8,128)(2,1)S(1)}, u32[]{:S(2)}, u32[]{:S(2)}) collective-permute-start(bf16[16,256]{1,0:T(8,128)(2,1)S(1)} %shard_map.69), channel_id=1, source_target_pairs={{0,28},{4,24},{8,20},{12,16},{16,12},{20,8},{24,4},{28,0},{1,29},{... | collective-permute-start | bytes 24584 | tf_op jit(solution)/shard_map/ppermute | solution.py:168
  11.3 0.0 collective-permute-done.1.refs_1_
  11.3 0.9 %collective-permute-done.4.refs_3_ = bf16[16,256]{1,0:T(8,128)(2,1)S(1)} collective-permute-done((bf16[16,256]{1,0:T(8,128)(2,1)S(1)}, bf16[16,256]{1,0:T(8,128)(2,1)S(1)}, u32[]{:S(2)}, u32[]{:S(2)}) %collective-permute-start.4) | collective-permute-done | bytes 8224 | tf_op jit(solution)/shard_map/ppermute | solution.py:168
  12.2 1.6 %collective-permute-done.3.refs_2_ = bf16[16,256]{1,0:T(8,128)(2,1)S(1)} collective-permute-done((bf16[16,256]{1,0:T(8,128)(2,1)S(1)}, bf16[16,256]{1,0:T(8,128)(2,1)S(1)}, u32[]{:S(2)}, u32[]{:S(2)}) %collective-permute-start.3) | collective-permute-done | bytes 8224 | tf_op jit(solution)/shard_map/ppermute | solution.py:168
  13.8 0.8 %combine.1 = (bf16[1,2048]{1,0:T(2,128)(2,1)}, f32[1,16]{1,0:T(1,128)}) custom-call(bf16[16,256]{1,0:T(8,128)(2,1)S(1)} %shard_map.68.refs_0_, bf16[16,256]{1,0:T(8,128)(2,1)S(1)} %collective-permute-done.1.refs_1_, bf16[16,256]{1,0:T(8,128)(2,1)S(1)} %collective-permute-done.3.refs_2_, bf16[16,256]{1,0:T(8,128)(2,1)S(1)} %collective-permute-done.4.refs_3_), custom_call_target="tpu_custom_call" | custom-call | flops 65536 | bytes 8192 | tf_op jit(solution)/shard_map/combine/pallas_call | solution.py:144
  (3 shorter events, 0.0 us)
Async XLA Ops:
  0.6 0.8 %copy-start = (bf16[128,256]{1,0:T(8,128)(2,1)S(1)}, bf16[128,256]{1,0:T(8,128)(2,1)}, u32[]{:S(2)}) copy-start(bf16[128,256]{1,0:T(8,128)(2,1)} %keys_ref.1) | copy-start | bytes 196612
  1.5 0.8 %copy-start.1 = (bf16[128,256]{1,0:T(8,128)(2,1)S(1)}, bf16[128,256]{1,0:T(8,128)(2,1)}, u32[]{:S(2)}) copy-start(bf16[128,256]{1,0:T(8,128)(2,1)} %values_ref.1) | copy-start | bytes 196612
  2.3 0.7 %copy-start.3 = (s32[128]{0:T(128)S(1)}, s32[128]{0:T(128)}, u32[]{:S(2)}) copy-start(s32[128]{0:T(128)} %places_ref.1) | copy-start | bytes 1540
  3.0 0.7 %copy-start.2 = (bf16[1,2048]{1,0:T(2,128)(2,1)S(1)}, bf16[1,2048]{1,0:T(2,128)(2,1)}, u32[]{:S(2)}) copy-start(bf16[1,2048]{1,0:T(2,128)(2,1)} %query_ref.1) | copy-start | bytes 12292
  3.0 3.8 %collective-permute-start = (bf16[272,256]{1,0:T(8,128)(2,1)S(1)}, bf16[272,256]{1,0:T(8,128)(2,1)S(1)}, u32[]{:S(2)}, u32[]{:S(2)}) collective-permute-start(bf16[272,256]{1,0:T(8,128)(2,1)S(1)} %pack.1.refs_0_), channel_id=1, source_target_pairs={{0,8},{4,12},{8,0},{12,4},{16,24},{20,28},{24,16},{28,20},{1,9},{5... | collective-permute-start | bytes 417800 | tf_op jit(solution)/shard_map/ppermute | solution.py:168
  3.7 5.1 %collective-permute-start.2 = (bf16[1,2048]{1,0:T(2,128)(2,1)S(1)}, bf16[1,2048]{1,0:T(2,128)(2,1)S(1)}, u32[]{:S(2)}, u32[]{:S(2)}) collective-permute-start(bf16[1,2048]{1,0:T(2,128)(2,1)S(1)} %copy-done.2), channel_id=1, source_target_pairs={{0,24},{4,28},{8,16},{12,20},{16,8},{20,12},{24,0},{28,4},{1,25},{... | collective-permute-start | bytes 12296 | tf_op jit(solution)/shard_map/ppermute | solution.py:168
  7.2 4.1 %collective-permute-start.1 = (bf16[16,256]{1,0:T(8,128)(2,1)S(1)}, bf16[16,256]{1,0:T(8,128)(2,1)S(1)}, u32[]{:S(2)}, u32[]{:S(2)}) collective-permute-start(bf16[16,256]{1,0:T(8,128)(2,1)S(1)} %shard_map.68.refs_0_), channel_id=1, source_target_pairs={{0,4},{4,0},{8,12},{12,8},{16,20},{20,16},{24,28},{28,24},{1,5},{5... | collective-permute-start | bytes 24584 | tf_op jit(solution)/shard_map/ppermute | solution.py:168
  9.1 3.1 %collective-permute-start.4 = (bf16[16,256]{1,0:T(8,128)(2,1)S(1)}, bf16[16,256]{1,0:T(8,128)(2,1)S(1)}, u32[]{:S(2)}, u32[]{:S(2)}) collective-permute-start(bf16[16,256]{1,0:T(8,128)(2,1)S(1)} %shard_map.69), channel_id=1, source_target_pairs={{0,24},{4,28},{8,16},{12,20},{16,8},{20,12},{24,0},{28,4},{1,25},{... | collective-permute-start | bytes 24584 | tf_op jit(solution)/shard_map/ppermute | solution.py:168
  9.9 4.0 %collective-permute-start.3 = (bf16[16,256]{1,0:T(8,128)(2,1)S(1)}, bf16[16,256]{1,0:T(8,128)(2,1)S(1)}, u32[]{:S(2)}, u32[]{:S(2)}) collective-permute-start(bf16[16,256]{1,0:T(8,128)(2,1)S(1)} %shard_map.69), channel_id=1, source_target_pairs={{0,28},{4,24},{8,20},{12,16},{16,12},{20,8},{24,4},{28,0},{1,29},{... | collective-permute-start | bytes 24584 | tf_op jit(solution)/shard_map/ppermute | solution.py:168

commit v6 on v5

--- a/solution.py
+++ b/solution.py
@@ -12,7 +12,6 @@
 HD = 128
 HIDDEN = -1e30
 DIGIT_ROWS = 16
-STRETCH = 16
 VMEM_BYTES = 8 * 1024 * 1024
 
 
@@ -30,15 +29,6 @@
 
 def cost(flops):
     return pl.CostEstimate(flops=flops, bytes_accessed=flops // 8, transcendentals=0)
-
-
-def terms_of(column):
-    terms = []
-    for _ in range(3):
-        term = column.astype(jnp.bfloat16).astype(jnp.float32)
-        terms.append(term)
-        column = column - term
-    return terms
 
 
 def share_of(query, blocks, shown_rows):
@@ -75,11 +65,7 @@
     numerator = wide[:, :HD]
     for j in range(1, kv_heads):
         numerator = jnp.where(kv_of == j, wide[:, j * HD : (j + 1) * HD], numerator)
-    terms = [*terms_of(peak), *terms_of(denominator)]
-    stats = terms[-1]
-    for i in range(len(terms) - 2, -1, -1):
-        stats = jnp.where(lane < (i + 1) * STRETCH, terms[i], stats)
-    return jnp.concatenate([numerator, stats], axis=1).astype(jnp.bfloat16)
+    return jnp.concatenate([numerator, jnp.where(lane < HD // 2, peak, denominator)], axis=1)
 
 
 def tokens_kernel(owners, tokens_ref):
@@ -114,21 +100,17 @@
     refs[-1][...] = share_of(query_ref[...], blocks, shown)
 
 
-def stat_of(share, first):
-    at = HD + first * STRETCH
-    terms = [share[:, at + i * STRETCH : at + i * STRETCH + 1] for i in range(3)]
-    return terms[0] + terms[1] + terms[2]
-
-
 def combine_kernel(*refs):
-    shares = [r[...].astype(jnp.float32) for r in refs[:-2]]
+    shares = [r[...] for r in refs[:-2]]
     out_ref, peak_ref = refs[-2:]
     heads = shares[0].shape[0]
-    peaks = [stat_of(s, 0) for s in shares]
+    peaks = [s[:, HD : HD + 1] for s in shares]
     peak = functools.reduce(jnp.maximum, peaks)
     scales = [jnp.exp(p - peak) for p in peaks]
     numerator = sum(s[:, :HD] * c for s, c in zip(shares, scales, strict=True))
-    denominator = sum(stat_of(s, 3) * c for s, c in zip(shares, scales, strict=True))
+    denominator = sum(
+        s[:, HD + HD // 2 : HD + HD // 2 + 1] * c for s, c in zip(shares, scales, strict=True)
+    )
     out = (numerator / denominator).astype(jnp.bfloat16)
     for h in range(heads):
         out_ref[:, h * HD : (h + 1) * HD] = out[h : h + 1]
@@ -170,7 +152,7 @@
     def share(row, query):
         return pl.pallas_call(
             functools.partial(share_kernel, row),
-            out_shape=whole((heads, 2 * HD), jnp.bfloat16),
+            out_shape=whole((heads, 2 * HD), jnp.float32),
             in_specs=in_vmem(4),
             out_specs=in_vmem(1)[0],
             compiler_params=params(),

time: 15 us -> 14.9 us (level)
  no operation moved by 1% of the time
where the time goes in v6:
time: 14.9 us; the launch traced here: 14.7 us
  starting transfers between devices  6.78 us (46%)
  waiting for transfers between devices  2.63 us (18%)
  local copies, waits for them, and re-layouts  2.45 us (16%)
  Pallas kernels  1.48 us (10%)
  between operations  1.32 us (9%)
    ppermute x5, starting transfers between devices, swap(): return lax.ppermute(value, both, pairs)  6.78 us
    ppermute x5, waiting for transfers between devices, swap(): return lax.ppermute(value, both, pairs)  2.63 us
    unnamed x8, local copies, waits for them, and re-layouts  2.45 us
    pallas_call x1, Pallas kernels, combine(): pl.pallas_call(combine_kernel, out_shape=(whole((1, columns), jnp.bfloat1...  0.77 us
    pallas_call x2, Pallas kernels, share(): pl.pallas_call(functools.partial(share_kernel, row), out_shape=whole((hea...  0.69 us
  transfers between devices with their start and end apart: 5, of which 2 were waited for; matrix products, arithmetic and copies ran while one was open for 0% of the time, Pallas kernels for 5%

profile of v6, /device:TPU:0, one launch (start us, length us, event | category | flops | bytes accessed | tf_op | source)
XLA Modules:
  0.0 14.7 jit_solution(10665477740463226740)
XLA Ops:
  0.6 0.0 copy-start
  0.6 0.8 %copy-done = bf16[128,256]{1,0:T(8,128)(2,1)S(1)} copy-done((bf16[128,256]{1,0:T(8,128)(2,1)S(1)}, bf16[128,256]{1,0:T(8,128)(2,1)}, u32[]{:S(2)}) %copy-start) | copy-done | bytes 65560
  1.5 0.0 copy-start.1
  1.5 0.8 %copy-done.1 = bf16[128,256]{1,0:T(8,128)(2,1)S(1)} copy-done((bf16[128,256]{1,0:T(8,128)(2,1)S(1)}, bf16[128,256]{1,0:T(8,128)(2,1)}, u32[]{:S(2)}) %copy-start.1) | copy-done | bytes 65560
  2.3 0.0 copy-start.3
  2.3 0.7 %copy-done.3 = s32[128]{0:T(128)S(1)} copy-done((s32[128]{0:T(128)S(1)}, s32[128]{0:T(128)}, u32[]{:S(2)}) %copy-start.3) | copy-done | bytes 536
  3.0 0.0 copy-start.2
  3.0 0.6 %collective-permute-start = (bf16[272,256]{1,0:T(8,128)(2,1)S(1)}, bf16[272,256]{1,0:T(8,128)(2,1)S(1)}, u32[]{:S(2)}, u32[]{:S(2)}) collective-permute-start(bf16[272,256]{1,0:T(8,128)(2,1)S(1)} %pack.1.refs_0_), channel_id=1, source_target_pairs={{0,8},{4,12},{8,0},{12,4},{16,24},{20,28},{24,16},{28,20},{1,9},{5... | collective-permute-start | bytes 417800 | tf_op jit(solution)/shard_map/ppermute | solution.py:150
  3.5 0.1 copy-done.2
  3.7 2.5 %collective-permute-start.2 = (bf16[1,2048]{1,0:T(2,128)(2,1)S(1)}, bf16[1,2048]{1,0:T(2,128)(2,1)S(1)}, u32[]{:S(2)}, u32[]{:S(2)}) collective-permute-start(bf16[1,2048]{1,0:T(2,128)(2,1)S(1)} %copy-done.2), channel_id=1, source_target_pairs={{0,24},{4,28},{8,16},{12,20},{16,8},{20,12},{24,0},{28,4},{1,25},{... | collective-permute-start | bytes 12296 | tf_op jit(solution)/shard_map/ppermute | solution.py:150
  6.8 0.0 collective-permute-done.refs_1_
  6.8 0.3 %shard_map.68.refs_0_ = f32[16,256]{1,0:T(8,128)S(1)} custom-call(s32[2,128]{1,0:T(2,128)S(1)} %clock.1.clock_ref, bf16[1,2048]{1,0:T(2,128)(2,1)S(1)} %copy-done.2, bf16[272,256]{1,0:T(8,128)(2,1)S(1)} %pack.1.refs_0_, bf16[272,256]{1,0:T(8,128)(2,1)S(1)} %collective-permute-done.refs_1_), custom_call_target="tpu_custom_call" | custom-call | flops 4194304 | bytes 524288 | tf_op jit(solution)/shard_map/pallas_call | solution.py:153
  7.2 1.5 %collective-permute-start.1 = (f32[16,256]{1,0:T(8,128)S(1)}, f32[16,256]{1,0:T(8,128)S(1)}, u32[]{:S(2)}, u32[]{:S(2)}) collective-permute-start(f32[16,256]{1,0:T(8,128)S(1)} %shard_map.68.refs_0_), channel_id=1, source_target_pairs={{0,4},{4,0},{8,12},{12,8},{16,20},{20,16},{24,28},{28,24},{1,5},{5... | collective-permute-start | bytes 49160 | tf_op jit(solution)/shard_map/ppermute | solution.py:150
  8.7 0.0 collective-permute-done.2.query_ref
  8.7 0.3 %shard_map.69 = f32[16,256]{1,0:T(8,128)S(1)} custom-call(s32[2,128]{1,0:T(2,128)S(1)} %clock.1.clock_ref, bf16[1,2048]{1,0:T(2,128)(2,1)S(1)} %collective-permute-done.2.query_ref, bf16[272,256]{1,0:T(8,128)(2,1)S(1)} %pack.1.refs_0_, bf16[272,256]{1,0:T(8,128)(2,1)S(1)} %collective-permute-done.refs_1_), custom_call_target="tpu_custom_call" | custom-call | flops 4194304 | bytes 524288 | tf_op jit(solution)/shard_map/pallas_call | solution.py:153
  9.0 0.8 %collective-permute-start.4 = (f32[16,256]{1,0:T(8,128)S(1)}, f32[16,256]{1,0:T(8,128)S(1)}, u32[]{:S(2)}, u32[]{:S(2)}) collective-permute-start(f32[16,256]{1,0:T(8,128)S(1)} %shard_map.69), channel_id=1, source_target_pairs={{0,24},{4,28},{8,16},{12,20},{16,8},{20,12},{24,0},{28,4},{1,25},{... | collective-permute-start | bytes 49160 | tf_op jit(solution)/shard_map/ppermute | solution.py:150
  9.8 1.4 %collective-permute-start.3 = (f32[16,256]{1,0:T(8,128)S(1)}, f32[16,256]{1,0:T(8,128)S(1)}, u32[]{:S(2)}, u32[]{:S(2)}) collective-permute-start(f32[16,256]{1,0:T(8,128)S(1)} %shard_map.69), channel_id=1, source_target_pairs={{0,28},{4,24},{8,20},{12,16},{16,12},{20,8},{24,4},{28,0},{1,29},{... | collective-permute-start | bytes 49160 | tf_op jit(solution)/shard_map/ppermute | solution.py:150
  11.3 0.0 collective-permute-done.1.refs_1_
  11.3 1.0 %collective-permute-done.4.refs_3_ = f32[16,256]{1,0:T(8,128)S(1)} collective-permute-done((f32[16,256]{1,0:T(8,128)S(1)}, f32[16,256]{1,0:T(8,128)S(1)}, u32[]{:S(2)}, u32[]{:S(2)}) %collective-permute-start.4) | collective-permute-done | bytes 16416 | tf_op jit(solution)/shard_map/ppermute | solution.py:150
  12.2 1.7 %collective-permute-done.3.refs_2_ = f32[16,256]{1,0:T(8,128)S(1)} collective-permute-done((f32[16,256]{1,0:T(8,128)S(1)}, f32[16,256]{1,0:T(8,128)S(1)}, u32[]{:S(2)}, u32[]{:S(2)}) %collective-permute-start.3) | collective-permute-done | bytes 16416 | tf_op jit(solution)/shard_map/ppermute | solution.py:150
  13.9 0.8 %combine.1 = (bf16[1,2048]{1,0:T(2,128)(2,1)}, f32[1,16]{1,0:T(1,128)}) custom-call(f32[16,256]{1,0:T(8,128)S(1)} %shard_map.68.refs_0_, f32[16,256]{1,0:T(8,128)S(1)} %collective-permute-done.1.refs_1_, f32[16,256]{1,0:T(8,128)S(1)} %collective-permute-done.3.refs_2_, f32[16,256]{1,0:T(8,128)S(1)} %collective-permute-done.4.refs_3_), custom_call_target="tpu_custom_call" | custom-call | flops 65536 | bytes 8192 | tf_op jit(solution)/shard_map/combine/pallas_call | solution.py:126
  (3 shorter events, 0.0 us)
Async XLA Ops:
  0.6 0.8 %copy-start = (bf16[128,256]{1,0:T(8,128)(2,1)S(1)}, bf16[128,256]{1,0:T(8,128)(2,1)}, u32[]{:S(2)}) copy-start(bf16[128,256]{1,0:T(8,128)(2,1)} %keys_ref.1) | copy-start | bytes 196612
  1.5 0.8 %copy-start.1 = (bf16[128,256]{1,0:T(8,128)(2,1)S(1)}, bf16[128,256]{1,0:T(8,128)(2,1)}, u32[]{:S(2)}) copy-start(bf16[128,256]{1,0:T(8,128)(2,1)} %values_ref.1) | copy-start | bytes 196612
  2.3 0.7 %copy-start.3 = (s32[128]{0:T(128)S(1)}, s32[128]{0:T(128)}, u32[]{:S(2)}) copy-start(s32[128]{0:T(128)} %places_ref.1) | copy-start | bytes 1540
  3.0 0.7 %copy-start.2 = (bf16[1,2048]{1,0:T(2,128)(2,1)S(1)}, bf16[1,2048]{1,0:T(2,128)(2,1)}, u32[]{:S(2)}) copy-start(bf16[1,2048]{1,0:T(2,128)(2,1)} %query_ref.1) | copy-start | bytes 12292
  3.0 3.8 %collective-permute-start = (bf16[272,256]{1,0:T(8,128)(2,1)S(1)}, bf16[272,256]{1,0:T(8,128)(2,1)S(1)}, u32[]{:S(2)}, u32[]{:S(2)}) collective-permute-start(bf16[272,256]{1,0:T(8,128)(2,1)S(1)} %pack.1.refs_0_), channel_id=1, source_target_pairs={{0,8},{4,12},{8,0},{12,4},{16,24},{20,28},{24,16},{28,20},{1,9},{5... | collective-permute-start | bytes 417800 | tf_op jit(solution)/shard_map/ppermute | solution.py:150
  3.7 5.0 %collective-permute-start.2 = (bf16[1,2048]{1,0:T(2,128)(2,1)S(1)}, bf16[1,2048]{1,0:T(2,128)(2,1)S(1)}, u32[]{:S(2)}, u32[]{:S(2)}) collective-permute-start(bf16[1,2048]{1,0:T(2,128)(2,1)S(1)} %copy-done.2), channel_id=1, source_target_pairs={{0,24},{4,28},{8,16},{12,20},{16,8},{20,12},{24,0},{28,4},{1,25},{... | collective-permute-start | bytes 12296 | tf_op jit(solution)/shard_map/ppermute | solution.py:150
  7.2 4.1 %collective-permute-start.1 = (f32[16,256]{1,0:T(8,128)S(1)}, f32[16,256]{1,0:T(8,128)S(1)}, u32[]{:S(2)}, u32[]{:S(2)}) collective-permute-start(f32[16,256]{1,0:T(8,128)S(1)} %shard_map.68.refs_0_), channel_id=1, source_target_pairs={{0,4},{4,0},{8,12},{12,8},{16,20},{20,16},{24,28},{28,24},{1,5},{5... | collective-permute-start | bytes 49160 | tf_op jit(solution)/shard_map/ppermute | solution.py:150
  9.0 3.2 %collective-permute-start.4 = (f32[16,256]{1,0:T(8,128)S(1)}, f32[16,256]{1,0:T(8,128)S(1)}, u32[]{:S(2)}, u32[]{:S(2)}) collective-permute-start(f32[16,256]{1,0:T(8,128)S(1)} %shard_map.69), channel_id=1, source_target_pairs={{0,24},{4,28},{8,16},{12,20},{16,8},{20,12},{24,0},{28,4},{1,25},{... | collective-permute-start | bytes 49160 | tf_op jit(solution)/shard_map/ppermute | solution.py:150
  9.8 4.1 %collective-permute-start.3 = (f32[16,256]{1,0:T(8,128)S(1)}, f32[16,256]{1,0:T(8,128)S(1)}, u32[]{:S(2)}, u32[]{:S(2)}) collective-permute-start(f32[16,256]{1,0:T(8,128)S(1)} %shard_map.69), channel_id=1, source_target_pairs={{0,28},{4,24},{8,20},{12,16},{16,12},{20,8},{24,4},{28,0},{1,29},{... | collective-permute-start | bytes 49160 | tf_op jit(solution)/shard_map/ppermute | solution.py:150

commit v7 on v6

--- a/solution.py
+++ b/solution.py
@@ -104,12 +104,15 @@
     shares = [r[...] for r in refs[:-2]]
     out_ref, peak_ref = refs[-2:]
     heads = shares[0].shape[0]
-    peaks = [s[:, HD : HD + 1] for s in shares]
+    left = lax.broadcasted_iota(jnp.int32, (heads, HD), 1) < HD // 2
+    stats = [s[:, HD:] for s in shares]
+    turned = [pltpu.roll(s, HD // 2, 1) for s in stats]
+    peaks = [jnp.where(left, s, t) for s, t in zip(stats, turned, strict=True)]
     peak = functools.reduce(jnp.maximum, peaks)
     scales = [jnp.exp(p - peak) for p in peaks]
     numerator = sum(s[:, :HD] * c for s, c in zip(shares, scales, strict=True))
     denominator = sum(
-        s[:, HD + HD // 2 : HD + HD // 2 + 1] * c for s, c in zip(shares, scales, strict=True)
+        jnp.where(left, t, s) * c for s, t, c in zip(stats, turned, scales, strict=True)
     )
     out = (numerator / denominator).astype(jnp.bfloat16)
     for h in range(heads):
@@ -117,7 +120,7 @@
     row = lax.broadcasted_iota(jnp.int32, (heads, heads), 0)
     column = lax.broadcasted_iota(jnp.int32, (heads, heads), 1)
     peak_ref[...] = jnp.sum(
-        jnp.where(row == column, peak, 0.0), axis=0, keepdims=True
+        jnp.where(row == column, peak[:, :heads], 0.0), axis=0, keepdims=True
     )
 
 

time: 14.9 us -> 14.9 us (level)
  no operation moved by 1% of the time
where the time goes in v7:
time: 14.9 us; the launch traced here: 14.6 us
  starting transfers between devices  6.78 us (46%)
  waiting for transfers between devices  2.63 us (18%)
  local copies, waits for them, and re-layouts  2.45 us (16%)
  Pallas kernels  1.42 us (10%)
  between operations  1.32 us (9%)
    ppermute x5, starting transfers between devices, swap(): return lax.ppermute(value, both, pairs)  6.78 us
    ppermute x5, waiting for transfers between devices, swap(): return lax.ppermute(value, both, pairs)  2.63 us
    unnamed x8, local copies, waits for them, and re-layouts  2.45 us
    pallas_call x1, Pallas kernels, combine(): pl.pallas_call(combine_kernel, out_shape=(whole((1, columns), jnp.bfloat1...  0.71 us
    pallas_call x2, Pallas kernels, share(): pl.pallas_call(functools.partial(share_kernel, row), out_shape=whole((hea...  0.69 us
  transfers between devices with their start and end apart: 5, of which 2 were waited for; matrix products, arithmetic and copies ran while one was open for 0% of the time, Pallas kernels for 5%

profile of v7, /device:TPU:0, one launch (start us, length us, event | category | flops | bytes accessed | tf_op | source)
XLA Modules:
  0.0 14.6 jit_solution(13825653072868665107)
XLA Ops:
  0.6 0.0 copy-start
  0.6 0.8 %copy-done = bf16[128,256]{1,0:T(8,128)(2,1)S(1)} copy-done((bf16[128,256]{1,0:T(8,128)(2,1)S(1)}, bf16[128,256]{1,0:T(8,128)(2,1)}, u32[]{:S(2)}) %copy-start) | copy-done | bytes 65560
  1.5 0.0 copy-start.1
  1.5 0.8 %copy-done.1 = bf16[128,256]{1,0:T(8,128)(2,1)S(1)} copy-done((bf16[128,256]{1,0:T(8,128)(2,1)S(1)}, bf16[128,256]{1,0:T(8,128)(2,1)}, u32[]{:S(2)}) %copy-start.1) | copy-done | bytes 65560
  2.3 0.0 copy-start.3
  2.3 0.7 %copy-done.3 = s32[128]{0:T(128)S(1)} copy-done((s32[128]{0:T(128)S(1)}, s32[128]{0:T(128)}, u32[]{:S(2)}) %copy-start.3) | copy-done | bytes 536
  3.0 0.0 copy-start.2
  3.0 0.6 %collective-permute-start = (bf16[272,256]{1,0:T(8,128)(2,1)S(1)}, bf16[272,256]{1,0:T(8,128)(2,1)S(1)}, u32[]{:S(2)}, u32[]{:S(2)}) collective-permute-start(bf16[272,256]{1,0:T(8,128)(2,1)S(1)} %pack.1.refs_0_), channel_id=1, source_target_pairs={{0,8},{4,12},{8,0},{12,4},{16,24},{20,28},{24,16},{28,20},{1,9},{5... | collective-permute-start | bytes 417800 | tf_op jit(solution)/shard_map/ppermute | solution.py:153
  3.5 0.1 copy-done.2
  3.7 2.5 %collective-permute-start.2 = (bf16[1,2048]{1,0:T(2,128)(2,1)S(1)}, bf16[1,2048]{1,0:T(2,128)(2,1)S(1)}, u32[]{:S(2)}, u32[]{:S(2)}) collective-permute-start(bf16[1,2048]{1,0:T(2,128)(2,1)S(1)} %copy-done.2), channel_id=1, source_target_pairs={{0,24},{4,28},{8,16},{12,20},{16,8},{20,12},{24,0},{28,4},{1,25},{... | collective-permute-start | bytes 12296 | tf_op jit(solution)/shard_map/ppermute | solution.py:153
  6.8 0.0 collective-permute-done.refs_1_
  6.8 0.3 %shard_map.68.refs_0_ = f32[16,256]{1,0:T(8,128)S(1)} custom-call(s32[2,128]{1,0:T(2,128)S(1)} %clock.1.clock_ref, bf16[1,2048]{1,0:T(2,128)(2,1)S(1)} %copy-done.2, bf16[272,256]{1,0:T(8,128)(2,1)S(1)} %pack.1.refs_0_, bf16[272,256]{1,0:T(8,128)(2,1)S(1)} %collective-permute-done.refs_1_), custom_call_target="tpu_custom_call" | custom-call | flops 4194304 | bytes 524288 | tf_op jit(solution)/shard_map/pallas_call | solution.py:156
  7.2 1.5 %collective-permute-start.1 = (f32[16,256]{1,0:T(8,128)S(1)}, f32[16,256]{1,0:T(8,128)S(1)}, u32[]{:S(2)}, u32[]{:S(2)}) collective-permute-start(f32[16,256]{1,0:T(8,128)S(1)} %shard_map.68.refs_0_), channel_id=1, source_target_pairs={{0,4},{4,0},{8,12},{12,8},{16,20},{20,16},{24,28},{28,24},{1,5},{5... | collective-permute-start | bytes 49160 | tf_op jit(solution)/shard_map/ppermute | solution.py:153
  8.7 0.0 collective-permute-done.2.query_ref
  8.7 0.3 %shard_map.69 = f32[16,256]{1,0:T(8,128)S(1)} custom-call(s32[2,128]{1,0:T(2,128)S(1)} %clock.1.clock_ref, bf16[1,2048]{1,0:T(2,128)(2,1)S(1)} %collective-permute-done.2.query_ref, bf16[272,256]{1,0:T(8,128)(2,1)S(1)} %pack.1.refs_0_, bf16[272,256]{1,0:T(8,128)(2,1)S(1)} %collective-permute-done.refs_1_), custom_call_target="tpu_custom_call" | custom-call | flops 4194304 | bytes 524288 | tf_op jit(solution)/shard_map/pallas_call | solution.py:156
  9.0 0.8 %collective-permute-start.4 = (f32[16,256]{1,0:T(8,128)S(1)}, f32[16,256]{1,0:T(8,128)S(1)}, u32[]{:S(2)}, u32[]{:S(2)}) collective-permute-start(f32[16,256]{1,0:T(8,128)S(1)} %shard_map.69), channel_id=1, source_target_pairs={{0,24},{4,28},{8,16},{12,20},{16,8},{20,12},{24,0},{28,4},{1,25},{... | collective-permute-start | bytes 49160 | tf_op jit(solution)/shard_map/ppermute | solution.py:153
  9.8 1.4 %collective-permute-start.3 = (f32[16,256]{1,0:T(8,128)S(1)}, f32[16,256]{1,0:T(8,128)S(1)}, u32[]{:S(2)}, u32[]{:S(2)}) collective-permute-start(f32[16,256]{1,0:T(8,128)S(1)} %shard_map.69), channel_id=1, source_target_pairs={{0,28},{4,24},{8,20},{12,16},{16,12},{20,8},{24,4},{28,0},{1,29},{... | collective-permute-start | bytes 49160 | tf_op jit(solution)/shard_map/ppermute | solution.py:153
  11.3 0.0 collective-permute-done.1.refs_1_
  11.3 1.0 %collective-permute-done.4.refs_3_ = f32[16,256]{1,0:T(8,128)S(1)} collective-permute-done((f32[16,256]{1,0:T(8,128)S(1)}, f32[16,256]{1,0:T(8,128)S(1)}, u32[]{:S(2)}, u32[]{:S(2)}) %collective-permute-start.4) | collective-permute-done | bytes 16416 | tf_op jit(solution)/shard_map/ppermute | solution.py:153
  12.2 1.7 %collective-permute-done.3.refs_2_ = f32[16,256]{1,0:T(8,128)S(1)} collective-permute-done((f32[16,256]{1,0:T(8,128)S(1)}, f32[16,256]{1,0:T(8,128)S(1)}, u32[]{:S(2)}, u32[]{:S(2)}) %collective-permute-start.3) | collective-permute-done | bytes 16416 | tf_op jit(solution)/shard_map/ppermute | solution.py:153
  13.9 0.7 %combine.1 = (bf16[1,2048]{1,0:T(2,128)(2,1)}, f32[1,16]{1,0:T(1,128)}) custom-call(f32[16,256]{1,0:T(8,128)S(1)} %shard_map.68.refs_0_, f32[16,256]{1,0:T(8,128)S(1)} %collective-permute-done.1.refs_1_, f32[16,256]{1,0:T(8,128)S(1)} %collective-permute-done.3.refs_2_, f32[16,256]{1,0:T(8,128)S(1)} %collective-permute-done.4.refs_3_), custom_call_target="tpu_custom_call" | custom-call | flops 65536 | bytes 8192 | tf_op jit(solution)/shard_map/combine/pallas_call | solution.py:129
  (3 shorter events, 0.0 us)
Async XLA Ops:
  0.6 0.8 %copy-start = (bf16[128,256]{1,0:T(8,128)(2,1)S(1)}, bf16[128,256]{1,0:T(8,128)(2,1)}, u32[]{:S(2)}) copy-start(bf16[128,256]{1,0:T(8,128)(2,1)} %keys_ref.1) | copy-start | bytes 196612
  1.5 0.8 %copy-start.1 = (bf16[128,256]{1,0:T(8,128)(2,1)S(1)}, bf16[128,256]{1,0:T(8,128)(2,1)}, u32[]{:S(2)}) copy-start(bf16[128,256]{1,0:T(8,128)(2,1)} %values_ref.1) | copy-start | bytes 196612
  2.3 0.7 %copy-start.3 = (s32[128]{0:T(128)S(1)}, s32[128]{0:T(128)}, u32[]{:S(2)}) copy-start(s32[128]{0:T(128)} %places_ref.1) | copy-start | bytes 1540
  3.0 0.7 %copy-start.2 = (bf16[1,2048]{1,0:T(2,128)(2,1)S(1)}, bf16[1,2048]{1,0:T(2,128)(2,1)}, u32[]{:S(2)}) copy-start(bf16[1,2048]{1,0:T(2,128)(2,1)} %query_ref.1) | copy-start | bytes 12292
  3.0 3.8 %collective-permute-start = (bf16[272,256]{1,0:T(8,128)(2,1)S(1)}, bf16[272,256]{1,0:T(8,128)(2,1)S(1)}, u32[]{:S(2)}, u32[]{:S(2)}) collective-permute-start(bf16[272,256]{1,0:T(8,128)(2,1)S(1)} %pack.1.refs_0_), channel_id=1, source_target_pairs={{0,8},{4,12},{8,0},{12,4},{16,24},{20,28},{24,16},{28,20},{1,9},{5... | collective-permute-start | bytes 417800 | tf_op jit(solution)/shard_map/ppermute | solution.py:153
  3.7 5.0 %collective-permute-start.2 = (bf16[1,2048]{1,0:T(2,128)(2,1)S(1)}, bf16[1,2048]{1,0:T(2,128)(2,1)S(1)}, u32[]{:S(2)}, u32[]{:S(2)}) collective-permute-start(bf16[1,2048]{1,0:T(2,128)(2,1)S(1)} %copy-done.2), channel_id=1, source_target_pairs={{0,24},{4,28},{8,16},{12,20},{16,8},{20,12},{24,0},{28,4},{1,25},{... | collective-permute-start | bytes 12296 | tf_op jit(solution)/shard_map/ppermute | solution.py:153
  7.2 4.1 %collective-permute-start.1 = (f32[16,256]{1,0:T(8,128)S(1)}, f32[16,256]{1,0:T(8,128)S(1)}, u32[]{:S(2)}, u32[]{:S(2)}) collective-permute-start(f32[16,256]{1,0:T(8,128)S(1)} %shard_map.68.refs_0_), channel_id=1, source_target_pairs={{0,4},{4,0},{8,12},{12,8},{16,20},{20,16},{24,28},{28,24},{1,5},{5... | collective-permute-start | bytes 49160 | tf_op jit(solution)/shard_map/ppermute | solution.py:153
  9.0 3.2 %collective-permute-start.4 = (f32[16,256]{1,0:T(8,128)S(1)}, f32[16,256]{1,0:T(8,128)S(1)}, u32[]{:S(2)}, u32[]{:S(2)}) collective-permute-start(f32[16,256]{1,0:T(8,128)S(1)} %shard_map.69), channel_id=1, source_target_pairs={{0,24},{4,28},{8,16},{12,20},{16,8},{20,12},{24,0},{28,4},{1,25},{... | collective-permute-start | bytes 49160 | tf_op jit(solution)/shard_map/ppermute | solution.py:153
  9.8 4.1 %collective-permute-start.3 = (f32[16,256]{1,0:T(8,128)S(1)}, f32[16,256]{1,0:T(8,128)S(1)}, u32[]{:S(2)}, u32[]{:S(2)}) collective-permute-start(f32[16,256]{1,0:T(8,128)S(1)} %shard_map.69), channel_id=1, source_target_pairs={{0,28},{4,24},{8,20},{12,16},{16,12},{20,8},{24,4},{28,0},{1,29},{... | collective-permute-start | bytes 49160 | tf_op jit(solution)/shard_map/ppermute | solution.py:153

commit v8 on v7

--- a/solution.py
+++ b/solution.py
@@ -100,11 +100,8 @@
     refs[-1][...] = share_of(query_ref[...], blocks, shown)
 
 
-def combine_kernel(*refs):
-    shares = [r[...] for r in refs[:-2]]
-    out_ref, peak_ref = refs[-2:]
-    heads = shares[0].shape[0]
-    left = lax.broadcasted_iota(jnp.int32, (heads, HD), 1) < HD // 2
+def merged(shares):
+    left = lax.broadcasted_iota(jnp.int32, (shares[0].shape[0], HD), 1) < HD // 2
     stats = [s[:, HD:] for s in shares]
     turned = [pltpu.roll(s, HD // 2, 1) for s in stats]
     peaks = [jnp.where(left, s, t) for s, t in zip(stats, turned, strict=True)]
@@ -114,6 +111,19 @@
     denominator = sum(
         jnp.where(left, t, s) * c for s, t, c in zip(stats, turned, scales, strict=True)
     )
+    return numerator, peak, denominator, left
+
+
+def merge_kernel(*refs):
+    numerator, peak, denominator, left = merged([r[...] for r in refs[:-1]])
+    refs[-1][...] = jnp.concatenate([numerator, jnp.where(left, peak, denominator)], axis=1)
+
+
+def combine_kernel(*refs):
+    shares = [r[...] for r in refs[:-2]]
+    out_ref, peak_ref = refs[-2:]
+    heads = shares[0].shape[0]
+    numerator, peak, denominator, _ = merged(shares)
     out = (numerator / denominator).astype(jnp.bfloat16)
     for h in range(heads):
         out_ref[:, h * HD : (h + 1) * HD] = out[h : h + 1]
@@ -195,8 +205,18 @@
     own_share = share(0, queries)
     across = swap(own_share, 0, 1)
     other_share = share(1, other_query)
-    shares = [own_share, across, swap(other_share, 3, 1), swap(other_share, 3, 0)]
-    return combine(shares, columns)
+    corner = swap(other_share, 3, 1)
+    near = swap(other_share, 3, 0)
+    gathered = pl.pallas_call(
+        merge_kernel,
+        out_shape=whole((heads, 2 * HD), jnp.float32),
+        in_specs=in_vmem(3),
+        out_specs=in_vmem(1)[0],
+        compiler_params=params(),
+        cost_estimate=cost(1 << 16),
+        name="merge",
+    )(own_share, across, corner)
+    return combine([gathered, near], columns)
 
 
 def grouped(queries, cache_keys, cache_values, cache_places, span_start):

time: 14.9 us -> 14.9 us (level)
  no operation moved by 1% of the time
where the time goes in v8:
time: 14.9 us; the launch traced here: 14.6 us
  starting transfers between devices  6.78 us (46%)
  waiting for transfers between devices  2.57 us (17%)
  local copies, waits for them, and re-layouts  2.45 us (16%)
  Pallas kernels  1.5 us (10%)
  between operations  1.32 us (9%)
    ppermute x5, starting transfers between devices, swap(): return lax.ppermute(value, both, pairs)  6.78 us
    ppermute x5, waiting for transfers between devices, swap(): return lax.ppermute(value, both, pairs)  2.57 us
    unnamed x8, local copies, waits for them, and re-layouts  2.45 us
    pallas_call x1, Pallas kernels, combine(): pl.pallas_call(combine_kernel, out_shape=(whole((1, columns), jnp.bfloat1...  0.7 us
    pallas_call x2, Pallas kernels, share(): pl.pallas_call(functools.partial(share_kernel, row), out_shape=whole((hea...  0.69 us
  transfers between devices with their start and end apart: 5, of which 2 were waited for; matrix products, arithmetic and copies ran while one was open for 0% of the time, Pallas kernels for 5%

profile of v8, /device:TPU:0, one launch (start us, length us, event | category | flops | bytes accessed | tf_op | source)
XLA Modules:
  0.0 14.6 jit_solution(958896075873353023)
XLA Ops:
  0.6 0.0 copy-start
  0.6 0.8 %copy-done = bf16[128,256]{1,0:T(8,128)(2,1)S(1)} copy-done((bf16[128,256]{1,0:T(8,128)(2,1)S(1)}, bf16[128,256]{1,0:T(8,128)(2,1)}, u32[]{:S(2)}) %copy-start) | copy-done | bytes 65560
  1.5 0.0 copy-start.1
  1.5 0.8 %copy-done.1 = bf16[128,256]{1,0:T(8,128)(2,1)S(1)} copy-done((bf16[128,256]{1,0:T(8,128)(2,1)S(1)}, bf16[128,256]{1,0:T(8,128)(2,1)}, u32[]{:S(2)}) %copy-start.1) | copy-done | bytes 65560
  2.3 0.0 copy-start.3
  2.3 0.7 %copy-done.3 = s32[128]{0:T(128)S(1)} copy-done((s32[128]{0:T(128)S(1)}, s32[128]{0:T(128)}, u32[]{:S(2)}) %copy-start.3) | copy-done | bytes 536
  3.0 0.0 copy-start.2
  3.0 0.6 %collective-permute-start = (bf16[272,256]{1,0:T(8,128)(2,1)S(1)}, bf16[272,256]{1,0:T(8,128)(2,1)S(1)}, u32[]{:S(2)}, u32[]{:S(2)}) collective-permute-start(bf16[272,256]{1,0:T(8,128)(2,1)S(1)} %pack.1.refs_0_), channel_id=1, source_target_pairs={{0,8},{4,12},{8,0},{12,4},{16,24},{20,28},{24,16},{28,20},{1,9},{5... | collective-permute-start | bytes 417800 | tf_op jit(solution)/shard_map/ppermute | solution.py:163
  3.5 0.1 copy-done.2
  3.7 2.5 %collective-permute-start.2 = (bf16[1,2048]{1,0:T(2,128)(2,1)S(1)}, bf16[1,2048]{1,0:T(2,128)(2,1)S(1)}, u32[]{:S(2)}, u32[]{:S(2)}) collective-permute-start(bf16[1,2048]{1,0:T(2,128)(2,1)S(1)} %copy-done.2), channel_id=1, source_target_pairs={{0,24},{4,28},{8,16},{12,20},{16,8},{20,12},{24,0},{28,4},{1,25},{... | collective-permute-start | bytes 12296 | tf_op jit(solution)/shard_map/ppermute | solution.py:163
  6.8 0.0 collective-permute-done.refs_1_
  6.8 0.3 %shard_map.68.refs_0_ = f32[16,256]{1,0:T(8,128)S(1)} custom-call(s32[2,128]{1,0:T(2,128)S(1)} %clock.1.clock_ref, bf16[1,2048]{1,0:T(2,128)(2,1)S(1)} %copy-done.2, bf16[272,256]{1,0:T(8,128)(2,1)S(1)} %pack.1.refs_0_, bf16[272,256]{1,0:T(8,128)(2,1)S(1)} %collective-permute-done.refs_1_), custom_call_target="tpu_custom_call" | custom-call | flops 4194304 | bytes 524288 | tf_op jit(solution)/shard_map/pallas_call | solution.py:166
  7.2 1.5 %collective-permute-start.1 = (f32[16,256]{1,0:T(8,128)S(1)}, f32[16,256]{1,0:T(8,128)S(1)}, u32[]{:S(2)}, u32[]{:S(2)}) collective-permute-start(f32[16,256]{1,0:T(8,128)S(1)} %shard_map.68.refs_0_), channel_id=1, source_target_pairs={{0,4},{4,0},{8,12},{12,8},{16,20},{20,16},{24,28},{28,24},{1,5},{5... | collective-permute-start | bytes 49160 | tf_op jit(solution)/shard_map/ppermute | solution.py:163
  8.7 0.0 collective-permute-done.2.query_ref
  8.7 0.3 %shard_map.69 = f32[16,256]{1,0:T(8,128)S(1)} custom-call(s32[2,128]{1,0:T(2,128)S(1)} %clock.1.clock_ref, bf16[1,2048]{1,0:T(2,128)(2,1)S(1)} %collective-permute-done.2.query_ref, bf16[272,256]{1,0:T(8,128)(2,1)S(1)} %pack.1.refs_0_, bf16[272,256]{1,0:T(8,128)(2,1)S(1)} %collective-permute-done.refs_1_), custom_call_target="tpu_custom_call" | custom-call | flops 4194304 | bytes 524288 | tf_op jit(solution)/shard_map/pallas_call | solution.py:166
  9.0 1.7 %collective-permute-start.3 = (f32[16,256]{1,0:T(8,128)S(1)}, f32[16,256]{1,0:T(8,128)S(1)}, u32[]{:S(2)}, u32[]{:S(2)}) collective-permute-start(f32[16,256]{1,0:T(8,128)S(1)} %shard_map.69), channel_id=1, source_target_pairs={{0,28},{4,24},{8,20},{12,16},{16,12},{20,8},{24,4},{28,0},{1,29},{... | collective-permute-start | bytes 49160 | tf_op jit(solution)/shard_map/ppermute | solution.py:163
  10.7 0.5 %collective-permute-start.4 = (f32[16,256]{1,0:T(8,128)S(1)}, f32[16,256]{1,0:T(8,128)S(1)}, u32[]{:S(2)}, u32[]{:S(2)}) collective-permute-start(f32[16,256]{1,0:T(8,128)S(1)} %shard_map.69), channel_id=1, source_target_pairs={{0,24},{4,28},{8,16},{12,20},{16,8},{20,12},{24,0},{28,4},{1,25},{... | collective-permute-start | bytes 49160 | tf_op jit(solution)/shard_map/ppermute | solution.py:163
  11.3 0.0 collective-permute-done.1.refs_1_
  11.3 1.9 %collective-permute-done.3.refs_2_ = f32[16,256]{1,0:T(8,128)S(1)} collective-permute-done((f32[16,256]{1,0:T(8,128)S(1)}, f32[16,256]{1,0:T(8,128)S(1)}, u32[]{:S(2)}, u32[]{:S(2)}) %collective-permute-start.3) | collective-permute-done | bytes 16416 | tf_op jit(solution)/shard_map/ppermute | solution.py:163
  13.1 0.1 merge.1.refs_0_
  13.2 0.7 %collective-permute-done.4.refs_1_ = f32[16,256]{1,0:T(8,128)S(1)} collective-permute-done((f32[16,256]{1,0:T(8,128)S(1)}, f32[16,256]{1,0:T(8,128)S(1)}, u32[]{:S(2)}, u32[]{:S(2)}) %collective-permute-start.4) | collective-permute-done | bytes 16416 | tf_op jit(solution)/shard_map/ppermute | solution.py:163
  13.9 0.7 %combine.1 = (bf16[1,2048]{1,0:T(2,128)(2,1)}, f32[1,16]{1,0:T(1,128)}) custom-call(f32[16,256]{1,0:T(8,128)S(1)} %merge.1.refs_0_, f32[16,256]{1,0:T(8,128)S(1)} %collective-permute-done.4.refs_1_), custom_call_target="tpu_custom_call" | custom-call | flops 65536 | bytes 8192 | tf_op jit(solution)/shard_map/combine/pallas_call | solution.py:139
  (3 shorter events, 0.0 us)
Async XLA Ops:
  0.6 0.8 %copy-start = (bf16[128,256]{1,0:T(8,128)(2,1)S(1)}, bf16[128,256]{1,0:T(8,128)(2,1)}, u32[]{:S(2)}) copy-start(bf16[128,256]{1,0:T(8,128)(2,1)} %keys_ref.1) | copy-start | bytes 196612
  1.5 0.8 %copy-start.1 = (bf16[128,256]{1,0:T(8,128)(2,1)S(1)}, bf16[128,256]{1,0:T(8,128)(2,1)}, u32[]{:S(2)}) copy-start(bf16[128,256]{1,0:T(8,128)(2,1)} %values_ref.1) | copy-start | bytes 196612
  2.3 0.7 %copy-start.3 = (s32[128]{0:T(128)S(1)}, s32[128]{0:T(128)}, u32[]{:S(2)}) copy-start(s32[128]{0:T(128)} %places_ref.1) | copy-start | bytes 1540
  3.0 0.7 %copy-start.2 = (bf16[1,2048]{1,0:T(2,128)(2,1)S(1)}, bf16[1,2048]{1,0:T(2,128)(2,1)}, u32[]{:S(2)}) copy-start(bf16[1,2048]{1,0:T(2,128)(2,1)} %query_ref.1) | copy-start | bytes 12292
  3.0 3.8 %collective-permute-start = (bf16[272,256]{1,0:T(8,128)(2,1)S(1)}, bf16[272,256]{1,0:T(8,128)(2,1)S(1)}, u32[]{:S(2)}, u32[]{:S(2)}) collective-permute-start(bf16[272,256]{1,0:T(8,128)(2,1)S(1)} %pack.1.refs_0_), channel_id=1, source_target_pairs={{0,8},{4,12},{8,0},{12,4},{16,24},{20,28},{24,16},{28,20},{1,9},{5... | collective-permute-start | bytes 417800 | tf_op jit(solution)/shard_map/ppermute | solution.py:163
  3.7 5.0 %collective-permute-start.2 = (bf16[1,2048]{1,0:T(2,128)(2,1)S(1)}, bf16[1,2048]{1,0:T(2,128)(2,1)S(1)}, u32[]{:S(2)}, u32[]{:S(2)}) collective-permute-start(bf16[1,2048]{1,0:T(2,128)(2,1)S(1)} %copy-done.2), channel_id=1, source_target_pairs={{0,24},{4,28},{8,16},{12,20},{16,8},{20,12},{24,0},{28,4},{1,25},{... | collective-permute-start | bytes 12296 | tf_op jit(solution)/shard_map/ppermute | solution.py:163
  7.2 4.1 %collective-permute-start.1 = (f32[16,256]{1,0:T(8,128)S(1)}, f32[16,256]{1,0:T(8,128)S(1)}, u32[]{:S(2)}, u32[]{:S(2)}) collective-permute-start(f32[16,256]{1,0:T(8,128)S(1)} %shard_map.68.refs_0_), channel_id=1, source_target_pairs={{0,4},{4,0},{8,12},{12,8},{16,20},{20,16},{24,28},{28,24},{1,5},{5... | collective-permute-start | bytes 49160 | tf_op jit(solution)/shard_map/ppermute | solution.py:163
  9.0 4.1 %collective-permute-start.3 = (f32[16,256]{1,0:T(8,128)S(1)}, f32[16,256]{1,0:T(8,128)S(1)}, u32[]{:S(2)}, u32[]{:S(2)}) collective-permute-start(f32[16,256]{1,0:T(8,128)S(1)} %shard_map.69), channel_id=1, source_target_pairs={{0,28},{4,24},{8,20},{12,16},{16,12},{20,8},{24,4},{28,0},{1,29},{... | collective-permute-start | bytes 49160 | tf_op jit(solution)/shard_map/ppermute | solution.py:163
  10.7 3.2 %collective-permute-start.4 = (f32[16,256]{1,0:T(8,128)S(1)}, f32[16,256]{1,0:T(8,128)S(1)}, u32[]{:S(2)}, u32[]{:S(2)}) collective-permute-start(f32[16,256]{1,0:T(8,128)S(1)} %shard_map.69), channel_id=1, source_target_pairs={{0,24},{4,28},{8,16},{12,20},{16,8},{20,12},{24,0},{28,4},{1,25},{... | collective-permute-start | bytes 49160 | tf_op jit(solution)/shard_map/ppermute | solution.py:163
